TPU v7x, 32 devices: a whole 2x2x4 slice. The times are simulated.
32 devices in a mesh: node: 8 (over z, y), feat: 4 (over x, core).
Axes of the slice: x: 2, y: 2, z: 4, core: 2. Of those that a mesh axis runs over, the one named last changes fastest.
Arguments:
- memory: float32 [8192, 172], P('node')
- last_update: int32 [8192], P('node'), may hold values from 6000 to 9999
- ev_time: int32 [16384], P(('node', 'feat')), may hold values from 10000 to 11999
- nbr_gap: int32 [16384, 10], P(('node', 'feat')), may hold values from 1 to 1999
- slot_rows: int32 [32, 1536], P(('node', 'feat')), may hold values from -1 to 1023, as said below
- slot_ref: int32 [16384, 12], P(('node', 'feat')), may hold values from 0 to 1535, as said below
- edge_feat: bfloat16 [16384, 256], P('node', 'feat'), may hold values from -6 to 6
- frequency: float32 [100], replicated, may hold values from 0.001 to 0.1
- phase_shift: float32 [100], replicated, may hold values from -3.140625 to 3.140625
- w_query: bfloat16 [272, 272], replicated, may hold values from -0.375 to 0.375
- w_key: bfloat16 [272, 272], replicated, may hold values from -0.375 to 0.375
- w_value: bfloat16 [272, 272], replicated, may hold values from -0.375 to 0.375
- w_merge: bfloat16 [444, 172], replicated, may hold values from -0.25 to 0.25
- b_merge: float32 [172], replicated, may hold values from -3 to 3
- w_out: bfloat16 [172, 172], replicated, may hold values from -0.4375 to 0.4375
- b_out: float32 [172], replicated, may hold values from -3 to 3
- w_input: float32 [3, 700, 172], P(None, None, 'feat'), may hold values from -0.21875 to 0.21875
- w_hidden: float32 [3, 172, 172], P(None, None, 'feat'), may hold values from -0.4375 to 0.4375
- gru_bias: float32 [4, 172], P(None, 'feat'), may hold values from -3 to 3
Outputs:
- embedding: bfloat16 [16384, 172], P(('node', 'feat'))
- new_memory: float32 [8192, 172], P('node', 'feat')
Inputs may be any that keep to these rules, and one draw needn't show every extreme that they name: `slot_rows`: row r lists the nodes read by events r * 512 to (r + 1) * 512 - 1: slot s asks owner s // 192 (an index along node) for one of its local rows, or holds -1. Within one owner's 192 slots the live ones come first and name distinct rows; every row has 1024 live slots. `slot_ref`: entries of event e name live slots of row e // 512 of slot_rows; every live slot is named by some event of its block.
All inputs are finite; a program needn't handle non-finite values.
Results may differ from a plain program's by a relative error of at most 0.01.
Values may be sent and summed in bfloat16 or wider, within the bound.
No kernel may reach another device: no remote copies, remote signals or barrier semaphores. Data moves between devices by JAX's collectives and lax.ppermute only.
A program may use at most 128 MiB of HBM per device.

v0:
```python
import math

import jax
import jax.numpy as jnp
from jax import lax
from jax.sharding import PartitionSpec as P

HEADS = 2


precise = lax.Precision.HIGHEST


def time_code(gap_vals, frequency, phase_shift):
    return jnp.cos(gap_vals[..., None] * frequency + phase_shift)


def embed_events(
    source,
    neighbors,
    gap_vals,
    frequency,
    phase_shift,
    w_query,
    w_key,
    w_value,
    w_merge,
    b_merge,
    w_out,
    b_out,
):
    event_count = source.shape[0]
    nbr_count = neighbors.shape[1]
    att_width = w_query.shape[0]
    head_size = att_width // HEADS
    still_code = jnp.broadcast_to(jnp.cos(phase_shift), (event_count, phase_shift.shape[0]))
    query_in = jnp.concatenate([source, still_code], 1).astype(jnp.bfloat16)
    key_in = jnp.concatenate([neighbors, time_code(gap_vals, frequency, phase_shift)], 2).astype(
        jnp.bfloat16
    )
    key_in = key_in.reshape(event_count * nbr_count, att_width)
    queries = jnp.dot(query_in, w_query, preferred_element_type=jnp.float32).reshape(
        event_count, HEADS, head_size
    )
    key_vecs = jnp.dot(key_in, w_key, preferred_element_type=jnp.float32).reshape(
        event_count, nbr_count, HEADS, head_size
    )
    values = jnp.dot(key_in, w_value, preferred_element_type=jnp.float32).reshape(
        event_count, nbr_count, HEADS, head_size
    )
    scores = jnp.einsum("ehd,ekhd->ehk", queries, key_vecs, precision=precise) / math.sqrt(
        head_size
    )
    weights = jax.nn.softmax(scores, axis=2)
    attended = jnp.einsum("ehk,ekhd->ehd", weights, values, precision=precise).reshape(
        event_count, att_width
    )
    merged = jnp.concatenate([attended, source], 1).astype(jnp.bfloat16)
    hidden = jax.nn.relu(
        jnp.dot(merged, w_merge, preferred_element_type=jnp.float32) + b_merge
    ).astype(jnp.bfloat16)
    return (jnp.dot(hidden, w_out, preferred_element_type=jnp.float32) + b_out).astype(jnp.bfloat16)


def build_messages(
    source, target, stamp_src, stamp_dst, ev_time, edge_rows, frequency, phase_shift
):
    code_src = time_code(ev_time - stamp_src, frequency, phase_shift)
    code_dst = time_code(ev_time - stamp_dst, frequency, phase_shift)
    wide_edges = edge_rows.astype(jnp.float32)
    to_source = jnp.concatenate([source, target, code_src, wide_edges], 1)
    to_target = jnp.concatenate([target, source, code_dst, wide_edges], 1)
    return jnp.concatenate([to_source, to_target], 0)


def gru_update(inputs, previous, own_cols, w_hidden, gru_bias):
    recurrent = jnp.einsum("rn,gnm->grm", previous, w_hidden, precision=precise)
    reset_gate = jax.nn.sigmoid(inputs[0] + recurrent[0] + gru_bias[0])
    update_gate = jax.nn.sigmoid(inputs[1] + recurrent[1] + gru_bias[1])
    candidate = jnp.tanh(inputs[2] + gru_bias[2] + reset_gate * (recurrent[2] + gru_bias[3]))
    return (1.0 - update_gate) * candidate + update_gate * own_cols


def take_rows(lookup, source_table, source_stamps):
    safe_ids = jnp.maximum(lookup, 0)
    picked = jnp.take(source_table, safe_ids, axis=0)
    found_stamps = jnp.take(source_stamps, safe_ids, axis=0).astype(jnp.float32)
    return (picked, found_stamps)


def sum_rows(lookup, source_vals, weights, total):
    sums = jax.ops.segment_sum(source_vals, lookup, num_segments=total)
    hit_counts = jax.ops.segment_sum(weights, lookup, num_segments=total)
    return (sums, hit_counts)


def per_device(
    memory,
    last_update,
    ev_time,
    nbr_gap,
    slot_rows,
    slot_ref,
    edge_feat,
    frequency,
    phase_shift,
    w_query,
    w_key,
    w_value,
    w_merge,
    b_merge,
    w_out,
    b_out,
    w_input,
    w_hidden,
    gru_bias,
):
    node_count = lax.axis_size("node")
    row_count = memory.shape[0]
    mem_width = memory.shape[1]
    slot_count = slot_rows.shape[1]
    per_owner = slot_count // node_count
    requested = lax.all_to_all(
        slot_rows.reshape(node_count, per_owner), "node", split_axis=0, concat_axis=0, tiled=True
    ).reshape(slot_count)
    found_rows, found_stamps = take_rows(requested, memory, last_update)
    fetched, fetched_stamps = (
        lax.all_to_all(
            found_rows.reshape(node_count, per_owner, mem_width),
            "node",
            split_axis=0,
            concat_axis=0,
            tiled=True,
        ),
        lax.all_to_all(
            found_stamps.reshape(node_count, per_owner),
            "node",
            split_axis=0,
            concat_axis=0,
            tiled=True,
        ),
    )
    fetched = fetched.reshape(slot_count, mem_width)
    fetched_stamps = fetched_stamps.reshape(slot_count)
    edge_rows = lax.all_to_all(edge_feat, "feat", split_axis=0, concat_axis=1, tiled=True)
    picked = jnp.take(fetched, slot_ref, axis=0)
    stamps = jnp.take(fetched_stamps, slot_ref[:, :2], axis=0)
    embedding = embed_events(
        picked[:, 0],
        picked[:, 2:],
        nbr_gap.astype(jnp.float32),
        frequency,
        phase_shift,
        w_query,
        w_key,
        w_value,
        w_merge,
        b_merge,
        w_out,
        b_out,
    )
    message_rows = build_messages(
        picked[:, 0],
        picked[:, 1],
        stamps[:, 0],
        stamps[:, 1],
        ev_time,
        edge_rows,
        frequency,
        phase_shift,
    )
    endpoints = jnp.concatenate([slot_ref[:, 0], slot_ref[:, 1]])
    unit_weights = jnp.ones(endpoints.shape, jnp.float32)
    width_cols = w_hidden.shape[2]
    own_cols = lax.dynamic_slice_in_dim(memory, lax.axis_index("feat") * width_cols, width_cols, 1)
    partner_rows = message_rows[:, mem_width:]
    slot_sums, slot_hits = sum_rows(endpoints, partner_rows, unit_weights, slot_count)
    back_sums, back_hits = (
        lax.all_to_all(
            slot_sums.reshape(node_count, per_owner, -1).astype(jnp.bfloat16),
            "node",
            split_axis=0,
            concat_axis=0,
            tiled=True,
        ).astype(jnp.float32),
        lax.all_to_all(
            slot_hits.reshape(node_count, per_owner).astype(jnp.bfloat16),
            "node",
            split_axis=0,
            concat_axis=0,
            tiled=True,
        ).astype(jnp.float32),
    )
    node_sums, node_hits = sum_rows(
        requested, back_sums.reshape(slot_count, -1), back_hits.reshape(slot_count), row_count
    )
    totals, touched = (
        lax.psum(node_sums.astype(jnp.bfloat16), "feat").astype(jnp.float32),
        lax.psum(node_hits.astype(jnp.bfloat16), "feat").astype(jnp.float32),
    )
    own_part = memory * (touched > 0.0).astype(jnp.float32)[:, None]
    averaged = jnp.concatenate([own_part, totals / jnp.maximum(touched, 1.0)[:, None]], 1)
    inputs = jnp.einsum("rn,gnm->grm", averaged, w_input, precision=precise)
    renewed = gru_update(inputs, memory, own_cols, w_hidden, gru_bias)
    new_memory = jnp.where((touched > 0.0)[:, None], renewed, own_cols)
    return (embedding, new_memory)


def solution(mesh):
    return jax.shard_map(
        per_device,
        mesh=mesh,
        in_specs=(
            P("node", None),
            P("node"),
            P(("node", "feat")),
            P(("node", "feat"), None),
            P(("node", "feat"), None),
            P(("node", "feat"), None),
            P("node", "feat"),
            P(),
            P(),
            P(),
            P(),
            P(),
            P(),
            P(),
            P(),
            P(),
            P(None, None, "feat"),
            P(None, None, "feat"),
            P(None, "feat"),
        ),
        out_specs=(P(("node", "feat"), None), P("node", "feat")),
        check_vma=False,
    )
```

profile of v0, /device:TPU:0, one launch (start us, length us, event | category | flops | bytes accessed | tf_op | source)
XLA Modules:
  0.0 273.8 jit_solution(2949874133486687902)
XLA Ops:
  8.6 7.3 %all-to-all-start = ((s32[8,1,192]{2,1,0:T(1,128)}), s32[8,1,192]{2,1,0:T(1,128)S(1)}, u32[]{:S(2)}, u32[]{:S(2)}) async-start(s32[8,1,192]{2,1,0:T(1,128)} %all_to_all.30), calls=%async_computation | async-start | bytes 16384 | tf_op jit(solution)/shard_map/all_to_all | solution.py:123
  17.6 4.9 %all-to-all-done = s32[8,1,192]{2,1,0:T(1,128)S(1)} async-done(((s32[8,1,192]{2,1,0:T(1,128)}), s32[8,1,192]{2,1,0:T(1,128)S(1)}, u32[]{:S(2)}, u32[]{:S(2)}) %all-to-all-start) | async-done | bytes 6176 | tf_op jit(solution)/shard_map/all_to_all | solution.py:123
  22.6 5.9 %gather_fusion.2 = s32[1536]{0:T(1024)S(1)} fusion(s32[1024]{0:T(1024)S(1)} %copy-done.1, s32[2048]{0:T(1024)S(1)} %pad_clamp_fusion), kind=kCustom, calls=%fused_computation.2 | custom fusion | bytes 18432 | tf_op jit(solution)/shard_map/jit(_take)/gather | solution.py:87
  29.2 3.3 %all-to-all-start.3 = ((f32[8,1,192]{2,1,0:T(1,128)}), f32[8,1,192]{2,1,0:T(1,128)S(1)}, u32[]{:S(2)}, u32[]{:S(2)}) async-start(f32[8,1,192]{2,1,0:T(1,128)} %copy.114), calls=%async_computation.3 | async-start | bytes 16384 | tf_op jit(solution)/shard_map/all_to_all | solution.py:135
  33.6 4.6 %gather_fusion = f32[1536,172]{1,0:T(8,128)} fusion(f32[1024,172]{1,0:T(8,128)S(1)} %copy.105, s32[2048]{0:T(1024)S(1)} %pad_clamp_fusion), kind=kCustom, calls=%fused_computation | custom fusion | bytes 2119680 | tf_op jit(solution)/shard_map/jit(_take)/gather | solution.py:86
  38.3 2.0 copy.106
  40.3 3.4 %all-to-all-start.4 = ((bf16[4,512,64]{1,2,0:T(8,128)(2,1)}), bf16[4,512,64]{1,2,0:T(8,128)(2,1)S(1)}, u32[]{:S(2)}, u32[]{:S(2)}) async-start(bf16[4,512,64]{1,2,0:T(8,128)(2,1)} %bitcast.126), calls=%async_computation.4 | async-start | bytes 524288 | tf_op jit(solution)/shard_map/all_to_all | solution.py:145
  43.7 1.3 broadcast_select_fusion.1
  45.0 4.7 %all-to-all-done.4 = bf16[4,512,64]{1,2,0:T(8,128)(2,1)S(1)} async-done(((bf16[4,512,64]{1,2,0:T(8,128)(2,1)}), bf16[4,512,64]{1,2,0:T(8,128)(2,1)S(1)}, u32[]{:S(2)}, u32[]{:S(2)}) %all-to-all-start.4) | async-done | bytes 262176 | tf_op jit(solution)/shard_map/all_to_all | solution.py:145
  49.7 5.9 %all-to-all-start.1 = ((f32[8,192,172]{1,2,0:T(8,128)}), f32[8,192,172]{1,2,0:T(8,128)S(1)}, u32[]{:S(2)}, u32[]{:S(2)}) async-start(f32[8,192,172]{1,2,0:T(8,128)} %broadcast_select_fusion.1), calls=%async_computation.1 | async-start | bytes 2883584 | tf_op jit(solution)/shard_map/all_to_all | solution.py:128
  56.5 1.1 reshape.155
  59.1 1.8 copy.111
  60.8 1.1 reshape.171
  62.0 6.3 %scatter_custom_fusion = f32[1536]{0:T(1024)S(1)} fusion(s32[1024]{0:T(1024)S(1)} %pad_add_fusion, f32[1024]{0:T(1024)S(1)} %broadcast.68, f32[]{:T(128)} %constant.55.clone.1), kind=kCustom, calls=%fused_computation.97 | custom fusion | flops 1024 | bytes 6148 | tf_op jit(solution)/shard_map/scatter-add | solution.py:93
  69.8 6.1 %gather_fusion.3 = f32[1024]{0:T(1024)S(1)} fusion(f32[1536]{0:T(1024)S(1)} %reshape.138, s32[1024]{0:T(1024)S(1)} %broadcast_clamp_fusion.1), kind=kCustom, calls=%fused_computation.3 | custom fusion | bytes 12288 | tf_op jit(solution)/shard_map/jit(_take)/gather | solution.py:147
  78.2 2.1 add_cosine_fusion.1
  80.4 1.8 convert_element_type.96
  82.2 7.3 %all-to-all-done.1 = f32[8,192,172]{1,2,0:T(8,128)S(1)} async-done(((f32[8,192,172]{1,2,0:T(8,128)}), f32[8,192,172]{1,2,0:T(8,128)S(1)}, u32[]{:S(2)}, u32[]{:S(2)}) %all-to-all-start.1) | async-done | bytes 1056800 | tf_op jit(solution)/shard_map/all_to_all | solution.py:128
  89.5 1.1 copy-done.5
  90.6 3.6 %all-to-all-start.2 = ((bf16[8,1,192]{2,1,0:T(2,128)(2,1)}), bf16[8,1,192]{2,1,0:T(2,128)(2,1)S(1)}, u32[]{:S(2)}, u32[]{:S(2)}) async-start(bf16[8,1,192]{2,1,0:T(2,128)(2,1)} %convert_element_type.97), calls=%async_computation.2 | async-start | bytes 16384 | tf_op jit(solution)/shard_map/all_to_all | solution.py:186
  94.2 1.9 copy.107
  96.2 23.7 %gather_fusion.1 = f32[6144,172]{1,0:T(8,128)} fusion(f32[1536,172]{1,0:T(8,128)S(1)} %bitcast.122, s32[6144]{0:T(1024)S(1)} %broadcast_clamp_fusion), kind=kCustom, calls=%fused_computation.1 | custom fusion | bytes 8478720 | tf_op jit(solution)/shard_map/jit(_take)/gather | solution.py:146
  119.9 8.3 %reshape.154 = f32[512,12,172]{2,1,0:T(8,128)} reshape(f32[6144,172]{1,0:T(8,128)} %gather_fusion.1) | data formatting | bytes 8454144 | tf_op jit(solution)/shard_map/jit(_take)/gather | solution.py:146
  128.2 9.0 %copy.109 = f32[512,12,172]{0,2,1:T(8,128)} copy(f32[512,12,172]{2,1,0:T(8,128)} %reshape.154) | data formatting | bytes 8454144 | tf_op jit(solution)/shard_map/jit(_take)/gather | solution.py:146
  137.3 2.8 %broadcast_select_fusion = f32[512,12,172]{0,2,1:T(8,128)S(1)} fusion(f32[512,12,172]{0,2,1:T(8,128)} %copy.109, pred[512,12]{0,1:T(8,128)(4,1)S(1)} %compare_and_fusion), kind=kLoop, calls=%fused_computation.26 | loop fusion | flops 1056768 | bytes 8460288 | tf_op jit(solution)/shard_map/jit(_take)/select_n | solution.py:146
  140.1 2.0 copy-done.2
  142.4 2.1 copy.116
  144.5 10.0 %scatter_custom_fusion.2 = f32[1536,528]{1,0:T(8,128)} fusion(s32[1024]{0:T(1024)} %copy-done.23, f32[1024,528]{1,0:T(8,128)} %copy.116, f32[]{:T(128)} %constant.55.clone.1), kind=kCustom, calls=%fused_computation.28 | custom fusion | flops 540672 | bytes 3244544 | tf_op jit(solution)/shard_map/scatter-add | solution.py:92
  154.5 3.1 %copy.117 = bf16[1536,528]{0,1:T(8,128)(2,1)S(1)} copy(f32[1536,528]{1,0:T(8,128)} %scatter_custom_fusion.2) | data formatting | bytes 4866048 | tf_op jit(solution)/shard_map/scatter-add | solution.py:92
  157.6 2.3 copy.134
  159.9 6.1 %all-to-all-start.5 = ((bf16[8,192,528]{2,1,0:T(8,128)(2,1)}), bf16[8,192,528]{2,1,0:T(8,128)(2,1)S(1)}, u32[]{:S(2)}, u32[]{:S(2)}) async-start(bf16[8,192,528]{2,1,0:T(8,128)(2,1)} %bitcast.23), calls=%async_computation.5 | async-start | bytes 3932160 | tf_op jit(solution)/shard_map/all_to_all | solution.py:179
  166.4 7.9 %cosine_convert_fusion = bf16[512,10,100]{0,2,1:T(8,128)(2,1)} fusion(f32[100]{0:T(128)S(1)} %copy-done.25, f32[100]{0:T(128)S(1)} %copy-done.27, f32[512,10]{0,1:T(8,128)S(1)} %copy-done.20), kind=kLoop, calls=%fused_computation.27 | loop fusion | flops 1536000 | bytes 1045280 | tf_op jit(solution)/shard_map/convert.8
  174.3 1.5 convolution_bitcast_fusion
  176.0 11.1 %scatter_custom_fusion.1 = f32[1024]{0:T(1024)S(1)} fusion(s32[1536]{0:T(1024)S(1)} %reshape.187, f32[1536]{0:T(1024)S(1)} %reshape.189, f32[]{:T(128)} %constant.55.clone.1), kind=kCustom, calls=%fused_computation.103 | custom fusion | flops 1536 | bytes 4100 | tf_op jit(solution)/shard_map/scatter-add | solution.py:93
  187.1 6.0 %psum.14 = bf16[1024]{0:T(1024)(128)(2,1)S(1)} all-reduce(bf16[1024]{0:T(1024)(128)(2,1)S(1)} %convert_element_type.82), channel_id=1, replica_groups=mesh['node'=8,'feat'=4] {'feat'}, use_global_device_ids=true, to_apply=%region_4.5 | all-reduce | flops 1024 | bytes 4096 | tf_op jit(solution)/shard_map/psum | solution.py:199
  194.0 2.4 slice.162
  196.5 1.3 fusion.58
  198.2 1.7 multiply_reduce_fusion.1
  200.1 11.1 %all-to-all-done.5 = bf16[8,192,528]{2,1,0:T(8,128)(2,1)S(1)} async-done(((bf16[8,192,528]{2,1,0:T(8,128)(2,1)}), bf16[8,192,528]{2,1,0:T(8,128)(2,1)S(1)}, u32[]{:S(2)}, u32[]{:S(2)}) %all-to-all-start.5) | async-done | bytes 1622048 | tf_op jit(solution)/shard_map/all_to_all | solution.py:179
  211.1 1.3 copy-done.3
  212.4 12.1 %scatter_custom_fusion.3 = f32[1024,528]{1,0:T(8,128)S(1)} fusion(s32[1536]{0:T(1024)S(1)} %reshape.187, bf16[1536,528]{1,0:T(8,128)(2,1)} %bitcast.123, f32[]{:T(128)} %constant.55.clone.1), kind=kCustom, calls=%fused_computation.10 | custom fusion | flops 1622016 | bytes 3784708 | tf_op jit(solution)/shard_map/scatter-add | solution.py:92
  224.5 1.5 copy.121
  226.1 3.6 %multiply_reduce_fusion = bf16[512,2,136]{0,2,1:T(8,128)(2,1)S(1)} fusion(f32[512,2,10]{0,1,2:T(2,128)S(1)} %broadcast_divide_fusion, bf16[2,136,272,1]{2,1,0,3:T(8,128)(2,1)S(1)} %bitcast.129, bf16[512,10,100]{0,2,1:T(8,128)(2,1)} %cosine_convert_fusion, bf16[512,10,172]{0,2,1:T(8,128)(2,1)} %copy-done.9), kind=kOutput, calls=%fused_computation.8 | convolution fusion | flops 765812736 | bytes 3252736 | tf_op jit(solution)/shard_map/dot_general | solution.py:48
  229.7 1.1 fusion.11
  230.8 30.4 %all-reduce.2.cloned.1.call-done = bf16[1024,528]{0,1:T(8,128)(2,1)} async-done(((bf16[1024,528]{0,1:T(8,128)(2,1)}), bf16[1024,528]{0,1:T(8,128)(2,1)}) %all-reduce.2.cloned.1.call-update) | async-done | bytes 1081360 | tf_op jit(solution)/shard_map/psum | solution.py:198
  261.2 1.5 convert_divide_fusion
  262.7 2.3 fusion.9
  265.0 1.9 fusion.29
  (117 shorter events, 13.4 us)
Async XLA Ops:
  7.2 255.6 %copy-start = (f32[3,700,43]{1,2,0:T(8,128)S(1)}, f32[3,700,43]{1,2,0:T(8,128)}, u32[]{:S(2)}) copy-start(f32[3,700,43]{1,2,0:T(8,128)} %param.35) | copy-start | bytes 1083604
  7.2 15.4 %copy-start.1 = (s32[1024]{0:T(1024)S(1)}, s32[1024]{0:T(1024)}, u32[]{:S(2)}) copy-start(s32[1024]{0:T(1024)} %param.20) | copy-start | bytes 12292
  8.6 13.8 %all-to-all-start = ((s32[8,1,192]{2,1,0:T(1,128)}), s32[8,1,192]{2,1,0:T(1,128)S(1)}, u32[]{:S(2)}, u32[]{:S(2)}) async-start(s32[8,1,192]{2,1,0:T(1,128)} %all_to_all.30), calls=%async_computation | async-start | bytes 16384 | tf_op jit(solution)/shard_map/all_to_all | solution.py:123
  22.6 9.9 %copy-start.18 = (s32[512,12]{0,1:T(8,128)S(1)}, s32[512,12]{0,1:T(8,128)}, u32[]{:S(2)}) copy-start(s32[512,12]{0,1:T(8,128)} %param.24) | copy-start | bytes 73732
  22.6 9.9 %copy-start.4 = (f32[1024,172]{0,1:T(8,128)S(1)}, f32[1024,172]{0,1:T(8,128)}, u32[]{:S(2)}) copy-start(f32[1024,172]{0,1:T(8,128)} %param.19) | copy-start | bytes 2113540
  22.6 10.3 %copy-start.13 = (bf16[2048,64]{0,1:T(8,128)(2,1)S(1)}, bf16[2048,64]{0,1:T(8,128)(2,1)}, u32[]{:S(2)}) copy-start(bf16[2048,64]{0,1:T(8,128)(2,1)} %param.25) | copy-start | bytes 786436
  29.2 11.1 %all-to-all-start.3 = ((f32[8,1,192]{2,1,0:T(1,128)}), f32[8,1,192]{2,1,0:T(1,128)S(1)}, u32[]{:S(2)}, u32[]{:S(2)}) async-start(f32[8,1,192]{2,1,0:T(1,128)} %copy.114), calls=%async_computation.3 | async-start | bytes 16384 | tf_op jit(solution)/shard_map/all_to_all | solution.py:135
  40.3 9.4 %all-to-all-start.4 = ((bf16[4,512,64]{1,2,0:T(8,128)(2,1)}), bf16[4,512,64]{1,2,0:T(8,128)(2,1)S(1)}, u32[]{:S(2)}, u32[]{:S(2)}) async-start(bf16[4,512,64]{1,2,0:T(8,128)(2,1)} %bitcast.126), calls=%async_computation.4 | async-start | bytes 524288 | tf_op jit(solution)/shard_map/all_to_all | solution.py:145
  44.9 12.7 %copy-start.15 = (bf16[272,272]{1,0:T(8,128)(2,1)S(1)}, bf16[272,272]{1,0:T(8,128)(2,1)}, u32[]{:S(2)}) copy-start(bf16[272,272]{1,0:T(8,128)(2,1)} %param.29) | copy-start | bytes 443908
  45.0 13.5 %copy-start.21 = (s32[512,10]{0,1:T(8,128)S(1)}, s32[512,10]{0,1:T(8,128)}, u32[]{:S(2)}) copy-start(s32[512,10]{0,1:T(8,128)} %param.22) | copy-start | bytes 61444
  45.0 24.0 %copy-start.24 = (f32[100]{0:T(128)S(1)}, f32[100]{0:T(128)}, u32[]{:S(2)}) copy-start(f32[100]{0:T(128)} %param.27) | copy-start | bytes 1204
  49.7 11.2 %copy-start.11 = (bf16[4,512,64]{1,2,0:T(8,128)(2,1)}, bf16[4,512,64]{1,2,0:T(8,128)(2,1)S(1)}, u32[]{:S(2)}) copy-start(bf16[4,512,64]{1,2,0:T(8,128)(2,1)S(1)} %all-to-all-done.4) | copy-start | bytes 786436
  49.7 39.8 %all-to-all-start.1 = ((f32[8,192,172]{1,2,0:T(8,128)}), f32[8,192,172]{1,2,0:T(8,128)S(1)}, u32[]{:S(2)}, u32[]{:S(2)}) async-start(f32[8,192,172]{1,2,0:T(8,128)} %broadcast_select_fusion.1), calls=%async_computation.1 | async-start | bytes 2883584 | tf_op jit(solution)/shard_map/all_to_all | solution.py:128
  62.0 7.7 %copy-start.23 = (s32[1024]{0:T(1024)}, s32[1024]{0:T(1024)S(1)}, u32[]{:S(2)}) copy-start(s32[1024]{0:T(1024)S(1)} %pad_add_fusion) | copy-start | bytes 12292
  69.8 8.4 %copy-start.28 = (s32[512]{0:T(512)S(1)}, s32[512]{0:T(512)}, u32[]{:S(2)}) copy-start(s32[512]{0:T(512)} %param.21) | copy-start | bytes 6148
  69.8 8.4 %copy-start.26 = (f32[100]{0:T(128)S(1)}, f32[100]{0:T(128)}, u32[]{:S(2)}) copy-start(f32[100]{0:T(128)} %param.26) | copy-start | bytes 1204
  89.5 1.1 copy-start.5
  90.6 69.3 %all-to-all-start.2 = ((bf16[8,1,192]{2,1,0:T(2,128)(2,1)}), bf16[8,1,192]{2,1,0:T(2,128)(2,1)S(1)}, u32[]{:S(2)}, u32[]{:S(2)}) async-start(bf16[8,1,192]{2,1,0:T(2,128)(2,1)} %convert_element_type.97), calls=%async_computation.2 | async-start | bytes 16384 | tf_op jit(solution)/shard_map/all_to_all | solution.py:186
  137.2 4.9 %copy-start.8 = (f32[4,512,64]{1,2,0:T(8,128)S(1)}, f32[4,512,64]{1,2,0:T(8,128)}, u32[]{:S(2)}) copy-start(f32[4,512,64]{1,2,0:T(8,128)} %convert_element_type.96) | copy-start | bytes 1572868
  137.3 4.9 %copy-start.12 = (f32[512,100]{0,1:T(8,128)S(1)}, f32[512,100]{0,1:T(8,128)}, u32[]{:S(2)}) copy-start(f32[512,100]{0,1:T(8,128)} %get-tuple-element.19) | copy-start | bytes 614404
  140.1 2.0 copy-start.2
  159.9 6.4 %copy-start.29 = (f32[4,43]{1,0:T(4,128)S(1)}, f32[4,43]{1,0:T(4,128)}, u32[]{:S(2)}) copy-start(f32[4,43]{1,0:T(4,128)} %param.37) | copy-start | bytes 2068
  159.9 6.5 %copy-start.20 = (f32[512,10]{0,1:T(8,128)S(1)}, f32[512,10]{0,1:T(8,128)}, u32[]{:S(2)}) copy-start(f32[512,10]{0,1:T(8,128)} %convert_element_type.75) | copy-start | bytes 61444
  159.9 6.5 %copy-start.25 = (f32[100]{0:T(128)S(1)}, f32[100]{0:T(128)}, u32[]{:S(2)}) copy-start(f32[100]{0:T(128)} %param.27) | copy-start | bytes 1204
  159.9 6.5 %copy-start.27 = (f32[100]{0:T(128)S(1)}, f32[100]{0:T(128)}, u32[]{:S(2)}) copy-start(f32[100]{0:T(128)} %param.26) | copy-start | bytes 1204
  159.9 14.4 %copy-start.19 = (f32[3,172,43]{1,2,0:T(8,128)S(1)}, f32[3,172,43]{1,2,0:T(8,128)}, u32[]{:S(2)}) copy-start(f32[3,172,43]{1,2,0:T(8,128)} %param.36) | copy-start | bytes 266260
  159.9 51.2 %all-to-all-start.5 = ((bf16[8,192,528]{2,1,0:T(8,128)(2,1)}), bf16[8,192,528]{2,1,0:T(8,128)(2,1)S(1)}, u32[]{:S(2)}, u32[]{:S(2)}) async-start(bf16[8,192,528]{2,1,0:T(8,128)(2,1)} %bitcast.23), calls=%async_computation.5 | async-start | bytes 3932160 | tf_op jit(solution)/shard_map/all_to_all | solution.py:179
  166.1 95.1 %all-reduce.2.cloned.1.call-start = ((), (), s32[]{:S(2)}) async-start(), calls=%async_computation.6 | async-start | bytes 2162688 | tf_op jit(solution)/shard_map/psum | solution.py:198
  194.0 3.7 %copy-start.14 = (bf16[272,272]{1,0:T(8,128)(2,1)S(1)}, bf16[272,272]{1,0:T(8,128)(2,1)}, u32[]{:S(2)}) copy-start(bf16[272,272]{1,0:T(8,128)(2,1)} %param.28) | copy-start | bytes 443908
  194.0 3.7 %copy-start.22 = (bf16[272]{0:T(512)(128)(2,1)S(1)}, bf16[272]{0:T(512)(128)(2,1)}, u32[]{:S(2)}) copy-start(bf16[272]{0:T(512)(128)(2,1)} %pad.17.clone) | copy-start | bytes 1636
  194.0 4.1 %copy-start.10 = (bf16[512,10,100]{0,2,1:T(8,128)(2,1)S(1)}, bf16[512,10,100]{0,2,1:T(8,128)(2,1)}, u32[]{:S(2)}) copy-start(bf16[512,10,100]{0,2,1:T(8,128)(2,1)} %cosine_convert_fusion) | copy-start | bytes 3072004
  194.0 4.1 %copy-start.17 = (bf16[272,272]{0,1:T(8,128)(2,1)S(1)}, bf16[272,272]{0,1:T(8,128)(2,1)}, u32[]{:S(2)}) copy-start(bf16[272,272]{0,1:T(8,128)(2,1)} %copy.110) | copy-start | bytes 443908
  196.5 3.5 %copy-start.9 = (bf16[512,10,172]{0,2,1:T(8,128)(2,1)}, bf16[512,10,172]{0,2,1:T(8,128)(2,1)S(1)}, u32[]{:S(2)}) copy-start(bf16[512,10,172]{0,2,1:T(8,128)(2,1)S(1)} %slice.162) | copy-start | bytes 5283844
  211.1 1.3 copy-start.3
  224.5 1.5 copy-start.16
  226.0 3.6 %copy-start.30 = (bf16[444,172]{0,1:T(8,128)(2,1)S(1)}, bf16[444,172]{0,1:T(8,128)(2,1)}, u32[]{:S(2)}) copy-start(bf16[444,172]{0,1:T(8,128)(2,1)} %param.31) | copy-start | bytes 458212
  226.0 3.6 %copy-start.31 = (bf16[172,172]{1,0:T(8,128)(2,1)S(1)}, bf16[172,172]{1,0:T(8,128)(2,1)}, u32[]{:S(2)}) copy-start(bf16[172,172]{1,0:T(8,128)(2,1)} %param.33) | copy-start | bytes 177508
  226.0 3.6 %copy-start.32 = (f32[172]{0:T(256)S(1)}, f32[172]{0:T(256)}, u32[]{:S(2)}) copy-start(f32[172]{0:T(256)} %param.34) | copy-start | bytes 2068
  226.0 3.6 %copy-start.33 = (f32[172]{0:T(256)S(1)}, f32[172]{0:T(256)}, u32[]{:S(2)}) copy-start(f32[172]{0:T(256)} %param.32) | copy-start | bytes 2068
  229.7 33.1 %copy-start.6 = (f32[1024,172]{0,1:T(8,128)S(1)}, f32[1024,172]{0,1:T(8,128)}, u32[]{:S(2)}) copy-start(f32[1024,172]{0,1:T(8,128)} %broadcast_multiply_fusion) | copy-start | bytes 2113540
  262.7 2.3 copy-start.7
Sparse Core Ops, SparseCore 0:
  226.1 35.0 all-reduce.1
where the time goes:
time: 275 us; the launch traced here: 274 us
  local copies, waits for them, and re-layouts  90.8 us (33%)
  other arithmetic  63.4 us (23%)
  waiting for transfers between devices  58.4 us (21%)
  starting transfers between devices  30 us (11%)
  between operations  14.7 us (5%)
  matrix products  10.6 us (4%)
  blocking collectives  5.97 us (2%)
    gather x3, local copies, waits for them, and re-layouts, per_device(): picked = jnp.take(fetched, slot_ref, axis=0)  41.1 us
    psum x1, waiting for transfers between devices, per_device(): lax.psum(node_sums.astype(jnp.bfloat16), 'feat').astype(jnp.float32)  30.4 us
    scatter-add x2, other arithmetic, sum_rows(): sums = jax.ops.segment_sum(source_vals, lookup, num_segments=total)  22 us
    scatter-add x2, other arithmetic, sum_rows(): hit_counts = jax.ops.segment_sum(weights, lookup, num_segments=total)  17.4 us
    all_to_all x1, waiting for transfers between devices, per_device(): lax.all_to_all(slot_sums.reshape(node_count, per_owner, -1).astype(jnp.bf...  11.1 us
    another operation x2, other arithmetic  7.95 us
    unnamed x72, local copies, waits for them, and re-layouts  7.64 us
    all_to_all x1, starting transfers between devices, per_device(): lax.all_to_all(slot_rows.reshape(node_count, per_owner), 'node', split_ax...  7.31 us
  transfers between devices with their start and end apart: 7, of which 5 were waited for; matrix products, arithmetic and copies ran while one was open for 49% of the time, Pallas kernels for 0%

commit v1 on v0

v1 whole, which is shorter than its diff:
```python
import functools
import math

import jax
import jax.numpy as jnp
from jax import lax
from jax.experimental import pallas as pl
from jax.experimental.pallas import tpu as pltpu
from jax.sharding import PartitionSpec as P

HEADS = 2
LANES = 128
HALF = 64
GROUP = 8
EVENT_TILE = 128
STAMP_SHIFT = 6
HIT_BASE = 32.0

bf16 = jnp.bfloat16
f32 = jnp.float32
exact = lax.Precision.HIGHEST


def rounded(count, step):
    return -(-count // step) * step


def cosine(x):
    turns = jnp.floor(x * (1.0 / math.pi) + 0.5)
    r = x - turns * 3.140625
    r = r - turns * 9.67502593994140625e-4
    r = r - turns * 1.509957990978376432e-7
    half = turns * 0.5
    sign = 1.0 - 4.0 * (half - jnp.floor(half))
    s = r * r
    poly = 1.0 / 479001600.0
    for coef in (-1.0 / 3628800.0, 1.0 / 40320.0, -1.0 / 720.0, 1.0 / 24.0, -0.5, 1.0):
        poly = poly * s + coef
    return poly * sign


def mm(a, b):
    return jnp.dot(a, b, preferred_element_type=f32)


def mm_nt(a, b):
    return lax.dot_general(a, b, (((1,), (1,)), ((), ())), preferred_element_type=f32)


def hot(mask):
    return jnp.where(mask, 1.0, 0.0).astype(bf16)


def iota(shape, axis):
    return lax.broadcasted_iota(jnp.int32, shape, axis)


PART, TIME_AT, EDGE_AT, COLS = 256, 256, 384, 640
PIECES = COLS // LANES
SPARE_ROWS = 16


def pack_kernel(mem, time, feat, feat_ref, edge_ref, w_ref, *out_refs):
    own, events = edge_ref.shape
    events = events // feat
    gates, width, raw = w_ref.shape
    lines = jnp.concatenate([w_ref[g] for g in range(gates)], 0)
    spare = gates * width - LANES
    lines = jnp.concatenate([lines, jnp.zeros((LANES + SPARE_ROWS - gates * width, raw), f32)], 0)
    height = lines.shape[0]
    fill = lambda count: jnp.zeros((height, count), f32)
    lines = jnp.concatenate(
        [
            lines[:, mem : 2 * mem],
            fill(PART - mem),
            lines[:, 2 * mem : 2 * mem + time],
            fill(LANES - time),
            lines[:, 2 * mem + time :],
        ],
        1,
    ).astype(bf16)
    edge_rows = own * events // LANES
    for k, out_ref in enumerate(out_refs):
        dest = lax.rem(feat_ref[0] + k, feat)
        block = edge_ref[:, pl.ds(pl.multiple_of(dest * events, LANES), events)]
        for c in range(events // LANES):
            out_ref[c * own : (c + 1) * own, :] = block[:, c * LANES : (c + 1) * LANES]
        for c in range(PIECES):
            at = edge_rows + c * height
            out_ref[at : at + height, :] = lines[:, c * LANES : (c + 1) * LANES]


def rows_kernel(feat, feat_ref, ids_ref, memory_ref, stamp_ref, out_ref):
    nodes, _, _ = out_ref.shape
    per_owner = ids_ref.shape[1]
    mem, rows = memory_ref.shape
    stamps = stamp_ref[...]
    high = lax.shift_right_logical(stamps, STAMP_SHIFT)
    low = stamps - lax.shift_left(high, STAMP_SHIFT)
    tail = jnp.concatenate([high, low, jnp.zeros((2 * LANES - mem - 2, rows), jnp.int32)], 0).astype(f32)
    table = jnp.concatenate([memory_ref[...], tail], 0).astype(bf16)
    wanted = jnp.concatenate([ids_ref[pl.ds(n * feat + feat_ref[0], 1), :] for n in range(nodes)], 0)
    columns = jnp.transpose(wanted)
    for n in range(nodes):
        picked = mm_nt(hot(columns[:, n : n + 1] == iota((per_owner, rows), 1)), table)
        out_ref[n, 0:per_owner, :] = picked[:, :LANES].astype(bf16)
        tail = picked[:, LANES : LANES + HALF]
        tail = jnp.concatenate([tail[: per_owner // 2], tail[per_owner // 2 :]], 1)
        room = out_ref.shape[1] - per_owner - per_owner // 2
        if room:
            tail = jnp.concatenate([tail, jnp.zeros((room, LANES), f32)], 0)
        out_ref[n, per_owner:, :] = tail.astype(bf16)


def message_kernel(mem, per_owner, feat, own, feat_ref, rows_ref, ref_ref, reft_ref, time_ref, freq_ref, phase_ref, *rest):
    pack_refs = rest[:feat]
    table_ref, out_ref, w_ref, x_ref, edge_ref = rest[feat:]
    nodes = rows_ref.shape[0]
    slots = nodes * per_owner
    events = ref_ref.shape[0]
    time = freq_ref.shape[1]
    source_of = [lax.rem(feat_ref[0] + feat - k, feat) for k in range(feat)]
    for n in range(nodes):
        at = n * per_owner
        table_ref[at : at + per_owner, 0:LANES] = rows_ref[n, 0:per_owner, :]
        tail = rows_ref[n, per_owner : per_owner + per_owner // 2, :].astype(f32)
        tail = jnp.concatenate([tail[:, :HALF], tail[:, HALF:]], 0)
        tail = jnp.concatenate([tail, jnp.zeros((per_owner, HALF), f32)], 1)
        table_ref[at : at + per_owner, LANES : 2 * LANES] = tail.astype(bf16)
    edge_rows = own * events // LANES
    height = LANES + SPARE_ROWS
    spare = []
    for k in range(feat):
        for c in range(PIECES):
            at = edge_rows + c * height
            w_ref[k * LANES : (k + 1) * LANES, c * LANES : (c + 1) * LANES] = pack_refs[k][at : at + LANES, :]
        spare.append(
            jnp.concatenate(
                [
                    pack_refs[k][edge_rows + c * height + LANES : edge_rows + (c + 1) * height, :].astype(f32)[0:1]
                    for c in range(PIECES)
                ],
                1,
            )
        )
        for c in range(events // LANES):
            edge_ref[pl.ds(pl.multiple_of(source_of[k] * own, own), own), c * LANES : (c + 1) * LANES] = pack_refs[k][
                c * own : (c + 1) * own, :
            ]
    spare = jnp.concatenate(spare + [jnp.zeros((SPARE_ROWS - feat, COLS), f32)], 0).astype(bf16)
    edges = edge_ref[...]
    table = table_ref[...]
    slot_of = iota((events, slots), 1)
    hot_src = hot(ref_ref[:, 0:1] == slot_of)
    hot_dst = hot(ref_ref[:, 1:2] == slot_of)
    source = mm(hot_src, table)
    target = mm(hot_dst, table)
    freq = freq_ref[...]
    phase = phase_ref[...]

    def code(rows):
        stamps = rows[:, mem : mem + 1] * float(1 << STAMP_SHIFT) + rows[:, mem + 1 : mem + 2]
        return cosine((time_ref[...].astype(f32) - stamps) * freq + phase).astype(bf16)

    code_src = code(source)
    code_dst = code(target)
    source = source.astype(bf16)
    target = target.astype(bf16)
    w_part = w_ref[:, 0:PART]
    w_time = w_ref[:, TIME_AT : TIME_AT + time]
    by_edge = lax.dot_general(edges, w_ref[:, EDGE_AT:COLS], (((0,), (1,)), ((), ())), preferred_element_type=f32)
    to_src = (mm_nt(target, w_part) + mm_nt(code_src, w_time) + by_edge).astype(bf16)
    to_dst = (mm_nt(source, w_part) + mm_nt(code_dst, w_time) + by_edge).astype(bf16)
    s_part, s_time, s_edge = spare[:, :PART], spare[:, TIME_AT : TIME_AT + time], spare[:, EDGE_AT:]
    line_edge = mm(s_edge, edges)
    ones = iota((SPARE_ROWS, events), 0) == feat
    line_src = jnp.where(ones, 1.0, mm_nt(s_part, target) + mm_nt(s_time, code_src) + line_edge).astype(bf16)
    line_dst = jnp.where(ones, 1.0, mm_nt(s_part, source) + mm_nt(s_time, code_dst) + line_edge).astype(bf16)
    lines = mm(line_src, hot_src) + mm(line_dst, hot_dst)
    x_ref[:, 0:slots] = lines[0:8]
    back_src = hot(iota((slots, events), 0) == reft_ref[0:1, :])
    back_dst = hot(iota((slots, events), 0) == reft_ref[1:2, :])
    sums = (mm(back_src, to_src) + mm(back_dst, to_dst)).astype(bf16)
    groups = -(-per_owner // LANES)
    row_id = iota((GROUP, LANES), 0)
    extra = out_ref.shape[1] - per_owner
    for n in range(nodes):
        at = n * per_owner
        blocks = []
        for c in range(groups):
            x = x_ref[:, at + c * LANES : at + (c + 1) * LANES]
            hits = x[feat : feat + 1, :]
            high = jnp.floor(hits * (1.0 / HIT_BASE))
            low = hits - high * HIT_BASE
            blocks.append((x, high, low))
        for k in range(feat):
            tail = [
                jnp.where(row_id == 0, x[k : k + 1, :], jnp.where(row_id == 1, high, jnp.where(row_id == 2, low, 0.0)))
                for x, high, low in blocks
            ]
            if extra > GROUP * groups:
                tail.append(jnp.zeros((extra - GROUP * groups, LANES), f32))
            dest = n * feat + source_of[k]
            out_ref[dest, 0:per_owner, :] = sums[at : at + per_owner, k * LANES : (k + 1) * LANES]
            out_ref[dest, per_owner:, :] = jnp.concatenate(tail, 0).astype(bf16)


def embed_kernel(mem, table_ref, ref_ref, gap_ref, freq_ref, phase_ref, wq_ref, wk_ref, wv_ref, wm_ref, bm_ref, wo_ref, bo_ref, out_ref, hot_ref, key_ref, prod_ref):
    tile, columns = ref_ref.shape
    nbrs = columns - 2
    slots = table_ref.shape[0]
    att = wq_ref.shape[0]
    head = att // HEADS
    slot_of = iota((tile, slots), 1)
    hot_ref[0:tile, :] = hot(ref_ref[:, 0:1] == slot_of)
    for k in range(nbrs):
        hot_ref[(k + 1) * tile : (k + 2) * tile, :] = hot(ref_ref[:, 2 + k : 3 + k] == slot_of)
    fetched = mm(hot_ref[...], table_ref[...])
    freq = freq_ref[...]
    phase = phase_ref[...]
    kept = iota((tile, LANES), 1) < mem - LANES
    for k in range(nbrs + 1):
        at = k * tile
        if k == 0:
            angle = jnp.broadcast_to(phase, (tile, 2 * LANES))
        else:
            angle = gap_ref[:, k - 1 : k].astype(f32) * freq + phase
        wave = cosine(angle)
        key_ref[at : at + tile, 0:LANES] = fetched[at : at + tile, :LANES].astype(bf16)
        key_ref[at : at + tile, LANES : 2 * LANES] = jnp.where(kept, fetched[at : at + tile, LANES:], wave[:, :LANES]).astype(bf16)
        key_ref[at : at + tile, 2 * LANES : att] = wave[:, LANES : att - LANES].astype(bf16)
    query = mm(key_ref[0:tile, :], wq_ref[...]) * (1.0 / math.sqrt(head))
    keys = mm(key_ref[tile:, :], wk_ref[...])
    values = mm(key_ref[tile:, :], wv_ref[...])
    for k in range(nbrs):
        prod_ref[k * tile : (k + 1) * tile, :] = keys[k * tile : (k + 1) * tile, :] * query
    prod = prod_ref[...]
    gather = hot((iota((att, LANES), 0) >= head).astype(jnp.int32) == (iota((att, LANES), 1) & 1))
    high = prod.astype(bf16)
    scores = mm(high, gather) + mm((prod - high.astype(f32)).astype(bf16), gather)
    parts = [scores[k * tile : (k + 1) * tile, :] for k in range(nbrs)]
    top = functools.reduce(jnp.maximum, parts)
    parts = [jnp.exp(s - top) for s in parts]
    scale = 1.0 / functools.reduce(jnp.add, parts)
    spread = hot(
        ((iota((LANES, att), 1) >= head).astype(jnp.int32) == (iota((LANES, att), 0) & 1)) & (iota((LANES, att), 0) < 4)
    )
    upper = iota((tile, LANES), 1) < 2
    attended = jnp.zeros((tile, att), f32)
    for k in range(nbrs):
        w = parts[k] * scale
        w_high = w.astype(bf16).astype(f32)
        w = jnp.where(upper, w_high, w - w_high).astype(bf16)
        attended = attended + mm(w, spread) * values[k * tile : (k + 1) * tile, :]
    merged = mm(attended.astype(bf16), wm_ref[0:att, :]) + mm(key_ref[0:tile, 0:mem], wm_ref[att : att + mem, :])
    hidden = jnp.maximum(merged + bm_ref[...], 0.0).astype(bf16)
    out_ref[...] = (mm(hidden, wo_ref[...]) + bo_ref[...]).astype(bf16)


def state_kernel(memory_ref, w_in_ref, w_hid_ref, bias_ref, out_ref):
    memory = memory_ref[...]
    mem = memory.shape[0]
    bias = bias_ref[...]

    def part(w, g):
        out_ref[g] = jnp.dot(w, memory, precision=exact, preferred_element_type=f32) + bias[:, g : g + 1]

    part(w_in_ref[0, :, 0:mem] + w_hid_ref[0], 0)
    part(w_in_ref[1, :, 0:mem] + w_hid_ref[1], 1)
    part(w_in_ref[2, :, 0:mem], 2)
    part(w_hid_ref[2], 3)


def update_kernel(per_owner, per_step, recv_ref, ids_ref, state_ref, own_ref, out_ref, acc_ref, turned_ref):
    rows = acc_ref.shape[0]
    width = own_ref.shape[0]
    groups = -(-per_owner // LANES)
    acc_ref[...] = jnp.zeros_like(acc_ref)

    def step(i, carry):
        main, side = [], []
        for b in range(per_step):
            block = i * per_step + b
            main.append(recv_ref[block, 0:per_owner, :])
            tail = recv_ref[block, per_owner:, :].astype(f32)
            for c in range(groups):
                count = min(LANES, per_owner - c * LANES)
                side.append(jnp.transpose(tail[c * GROUP : (c + 1) * GROUP, :])[:count, :])
        side = jnp.concatenate(side, 0)
        side = jnp.concatenate([side, jnp.zeros((side.shape[0], LANES - GROUP), f32)], 1).astype(bf16)
        data = jnp.concatenate([jnp.concatenate(main, 0), side], 1)
        ids = ids_ref[i]
        acc_ref[...] += mm(hot(iota((rows, ids.shape[1]), 0) == ids), data)
        return carry

    lax.fori_loop(0, recv_ref.shape[0] // per_step, step, 0)
    turned_ref[...] = jnp.transpose(acc_ref[...])
    at = 3 * width
    hits = turned_ref[at : at + 1, :] * HIT_BASE + turned_ref[at + 1 : at + 2, :]
    scale = 1.0 / jnp.maximum(hits, 1.0)
    own = own_ref[...]
    reset = jax.nn.sigmoid(turned_ref[0:width, :] * scale + state_ref[0])
    update = jax.nn.sigmoid(turned_ref[width : 2 * width, :] * scale + state_ref[1])
    fresh = jnp.tanh(turned_ref[2 * width : 3 * width, :] * scale + state_ref[2] + reset * state_ref[3])
    out_ref[...] = jnp.where(hits > 0.0, (1.0 - update) * fresh + update * own, own)


def cost(flops, moved):
    return pl.CostEstimate(flops=int(flops), transcendentals=0, bytes_accessed=int(moved))


def per_device(
    memory,
    last_update,
    ev_time,
    nbr_gap,
    slot_rows,
    slot_ref,
    edge_feat,
    frequency,
    phase_shift,
    w_query,
    w_key,
    w_value,
    w_merge,
    b_merge,
    w_out,
    b_out,
    w_input,
    w_hidden,
    gru_bias,
):
    nodes = lax.axis_size("node")
    feat = lax.axis_size("feat")
    blocks = nodes * feat
    rows, mem = memory.shape
    slots = slot_rows.shape[1]
    per_owner = slots // nodes
    events, columns = slot_ref.shape
    time = frequency.shape[0]
    att = w_query.shape[0]
    emb = w_out.shape[1]
    width = w_hidden.shape[2]
    everyone = ("node", "feat")

    asked = jnp.broadcast_to(slot_rows.reshape(nodes, 1, per_owner), (nodes, feat, per_owner)).reshape(blocks, 1, per_owner)
    asked = lax.all_to_all(asked, everyone, split_axis=0, concat_axis=0, tiled=True).reshape(blocks, per_owner)

    here = lax.axis_index("feat").astype(jnp.int32)
    here_line = here.reshape(1)
    memory_t = memory.T
    w_input_t = jnp.swapaxes(w_input, 1, 2)
    w_hidden_t = jnp.swapaxes(w_hidden, 1, 2)
    smem = pl.BlockSpec(memory_space=pltpu.SMEM)
    vmem = pl.BlockSpec(memory_space=pltpu.VMEM)

    own = edge_feat.shape[1]
    height = own * events // LANES + PIECES * (LANES + SPARE_ROWS)
    packed = pl.pallas_call(
        functools.partial(pack_kernel, mem, time, feat),
        in_specs=[smem, vmem, vmem],
        out_shape=[jax.ShapeDtypeStruct((height, LANES), bf16)] * feat,
        cost_estimate=cost(1e8, 1e6),
        name="pack",
    )(here_line, edge_feat.T, w_input_t)
    packed = [packed[0]] + [
        lax.ppermute(packed[k], "feat", [(i, (i + k) % feat) for i in range(feat)]) for k in range(1, feat)
    ]

    room = rounded(per_owner + per_owner // 2, 16)
    found = pl.pallas_call(
        functools.partial(rows_kernel, feat),
        out_shape=jax.ShapeDtypeStruct((nodes, room, LANES), bf16),
        in_specs=[smem, vmem, vmem, vmem],
        cost_estimate=cost(1e9, 2e6),
        name="rows",
    )(here_line, asked, memory_t, last_update.reshape(1, rows))
    found = lax.all_to_all(found, "node", split_axis=0, concat_axis=0, tiled=True)

    state = pl.pallas_call(
        state_kernel,
        out_shape=jax.ShapeDtypeStruct((4, width, rows), f32),
        cost_estimate=cost(3e9, 3e6),
        name="state",
    )(memory_t, w_input_t, w_hidden_t, gru_bias.T)

    freq_line = frequency.reshape(1, time)
    phase_line = phase_shift.reshape(1, time)
    groups = -(-per_owner // LANES)
    depth = per_owner + rounded(GROUP * groups, 16)
    fetched, sums = pl.pallas_call(
        functools.partial(message_kernel, mem, per_owner, feat, own),
        in_specs=[smem] + [vmem] * (6 + feat),
        out_shape=(
            jax.ShapeDtypeStruct((slots, 2 * LANES), bf16),
            jax.ShapeDtypeStruct((blocks, depth, LANES), bf16),
        ),
        scratch_shapes=[
            pltpu.VMEM((feat * LANES, COLS), bf16),
            pltpu.VMEM((8, rounded(slots, LANES) + LANES), f32),
            pltpu.VMEM((feat * own, events), bf16),
        ],
        cost_estimate=cost(4e9, 4e6),
        name="messages",
    )(here_line, found, slot_ref, slot_ref.T[:2], ev_time.reshape(events, 1), freq_line, phase_line, *packed)
    sums = lax.all_to_all(sums, everyone, split_axis=0, concat_axis=0, tiled=True)

    shift = mem - LANES
    spread = ((0, 0), (shift, 2 * LANES - shift - time))
    nbrs = columns - 2
    whole = lambda shape: pl.BlockSpec(shape, lambda i: (0,) * len(shape))
    embedding = pl.pallas_call(
        functools.partial(embed_kernel, mem),
        grid=(events // EVENT_TILE,),
        in_specs=[
            whole((slots, 2 * LANES)),
            pl.BlockSpec((EVENT_TILE, columns), lambda i: (i, 0)),
            pl.BlockSpec((EVENT_TILE, nbrs), lambda i: (i, 0)),
            whole((1, 2 * LANES)),
            whole((1, 2 * LANES)),
            whole((att, att)),
            whole((att, att)),
            whole((att, att)),
            whole((att + mem, emb)),
            whole((1, emb)),
            whole((emb, emb)),
            whole((1, emb)),
        ],
        out_specs=pl.BlockSpec((EVENT_TILE, emb), lambda i: (i, 0)),
        out_shape=jax.ShapeDtypeStruct((events, emb), bf16),
        scratch_shapes=[
            pltpu.VMEM(((nbrs + 1) * EVENT_TILE, slots), bf16),
            pltpu.VMEM(((nbrs + 1) * EVENT_TILE, att), bf16),
            pltpu.VMEM((nbrs * EVENT_TILE, att), f32),
        ],
        cost_estimate=cost(2e10, 4e6),
        name="embed",
    )(
        fetched,
        slot_ref,
        nbr_gap,
        jnp.pad(freq_line, spread),
        jnp.pad(phase_line, spread),
        w_query,
        w_key,
        w_value,
        w_merge,
        b_merge.reshape(1, emb),
        w_out,
        b_out.reshape(1, emb),
    )

    span = 768
    per_step = span // per_owner
    steps = blocks // per_step
    new_memory = pl.pallas_call(
        functools.partial(update_kernel, per_owner, per_step),
        out_shape=jax.ShapeDtypeStruct((width, rows), f32),
        scratch_shapes=[pltpu.VMEM((rows, 2 * LANES), f32), pltpu.VMEM((2 * LANES, rows), f32)],
        cost_estimate=cost(4e9, 4e6),
        name="update",
    )(
        sums,
        asked.reshape(steps, 1, per_step * per_owner),
        state,
        lax.dynamic_slice_in_dim(memory_t, here * width, width, 0),
    )
    return (embedding, new_memory.T)


def solution(mesh):
    return jax.shard_map(
        per_device,
        mesh=mesh,
        in_specs=(
            P("node", None),
            P("node"),
            P(("node", "feat")),
            P(("node", "feat"), None),
            P(("node", "feat"), None),
            P(("node", "feat"), None),
            P("node", "feat"),
            P(),
            P(),
            P(),
            P(),
            P(),
            P(),
            P(),
            P(),
            P(),
            P(None, None, "feat"),
            P(None, None, "feat"),
            P(None, "feat"),
        ),
        out_specs=(P(("node", "feat"), None), P("node", "feat")),
        check_vma=False,
    )
```

time: 275 us -> 106 us (0.39)
  local copies, waits for them, and re-layouts: 90.8 us -> 13.4 us
  other arithmetic: 63.4 us -> 0.79 us
  Pallas kernels: 0 us -> 56.1 us
  waiting for transfers between devices: 58.4 us -> 17.1 us
  between operations: 14.7 us -> 0.72 us
  starting transfers between devices: 30 us -> 17.4 us
  matrix products: 10.6 us -> 0 us
  blocking collectives: 5.97 us -> 0 us
    gather x9 -> x0, local copies, waits for them, and re-layouts: 60.6 us -> none  [the longest x3 41.1 us: per_device(): picked = jnp.take(fetched, slot_ref, axis=0)]
    pallas_call x0 -> x6, Pallas kernels: none -> 56.1 us  [the longest x1 30.2 us: per_device(): pl.pallas_call(functools.partial(embed_kernel, mem), grid=(events // EVEN...]
    scatter-add x4 -> x0, other arithmetic: 39.4 us -> none  [the longest x2 22 us: sum_rows(): sums = jax.ops.segment_sum(source_vals, lookup, num_segments=total)]
    psum x1 -> x0, waiting for transfers between devices: 30.4 us -> none  [per_device(): lax.psum(node_sums.astype(jnp.bfloat16), 'feat').astype(jnp.float32)]
    all_to_all x6 -> x3, waiting for transfers between devices: 28 us -> 9.36 us  [the longest x1 7.25 us: per_device(): lax.all_to_all(asked, everyone, split_axis=0, concat_axis=0, tiled=True)]
    all_to_all x6 -> x3, starting transfers between devices: 29.8 us -> 15.5 us  [the longest x1 7.33 us: per_device(): lax.all_to_all(asked, everyone, split_axis=0, concat_axis=0, tiled=True)]
    dot_general x6 -> x0, matrix products: 10.6 us -> none  [the longest x1 3.57 us: embed_events(): jnp.dot(key_in, w_value, preferred_element_type=jnp.float32)]
    another operation x2 -> x0, other arithmetic: 7.95 us -> none
  transfers between devices with their start and end apart: 7 -> 6, of which waited for: 5 -> 5; matrix products, arithmetic and copies ran while one was open for 49% -> 10% of each run, Pallas kernels for 0% -> 34%
where the time goes in v1:
time: 106 us
  Pallas kernels  56.1 us (53%)
  starting transfers between devices  17.4 us (16%)
  waiting for transfers between devices  17.1 us (16%)
  local copies, waits for them, and re-layouts  13.4 us (13%)
    pallas_call x1, Pallas kernels, per_device(): pl.pallas_call(functools.partial(embed_kernel, mem), grid=(events // EVEN...  30.2 us
    pallas_call x1, Pallas kernels, per_device(): pl.pallas_call(functools.partial(update_kernel, per_owner, per_step), out...  8.44 us
    ppermute x3, waiting for transfers between devices, per_device(): lax.ppermute(packed[k], 'feat', [(i, (i + k) % feat) for i in range(feat)])  7.77 us
    pallas_call x1, Pallas kernels, per_device(): pl.pallas_call(functools.partial(message_kernel, mem, per_owner, feat, ow...  7.65 us
    unnamed x30, local copies, waits for them, and re-layouts  7.64 us
    all_to_all x1, starting transfers between devices, per_device(): lax.all_to_all(asked, everyone, split_axis=0, concat_axis=0, tiled=True)  7.33 us
    all_to_all x1, waiting for transfers between devices, per_device(): lax.all_to_all(asked, everyone, split_axis=0, concat_axis=0, tiled=True)  7.25 us
    all_to_all x1, starting transfers between devices, per_device(): lax.all_to_all(sums, everyone, split_axis=0, concat_axis=0, tiled=True)  4.48 us
  transfers between devices with their start and end apart: 6, of which 5 were waited for; matrix products, arithmetic and copies ran while one was open for 10% of the time, Pallas kernels for 34%

profile of v1, /device:TPU:0, one launch (start us, length us, event | category | flops | bytes accessed | tf_op | source)
XLA Modules:
  0.0 105.6 jit_solution(5001557694063677738)
XLA Ops:
  0.6 0.7 reduce
  1.3 0.1 broadcast_in_dim.7
  1.4 0.7 reshape.34
  2.1 7.3 %all-to-all-start = ((s32[32,1,192]{2,1,0:T(1,128)}), s32[32,1,192]{2,1,0:T(1,128)S(1)}, u32[]{:S(2)}, u32[]{:S(2)}) async-start(s32[32,1,192]{2,1,0:T(1,128)} %reshape.34), calls=%async_computation | async-start | bytes 65536 | tf_op jit(solution)/shard_map/all_to_all | solution.py:347
  9.4 7.3 %all-to-all-done = s32[32,1,192]{2,1,0:T(1,128)S(1)} async-done(((s32[32,1,192]{2,1,0:T(1,128)}), s32[32,1,192]{2,1,0:T(1,128)S(1)}, u32[]{:S(2)}, u32[]{:S(2)}) %all-to-all-start) | async-done | bytes 24608 | tf_op jit(solution)/shard_map/all_to_all | solution.py:347
  16.7 0.6 copy.43
  17.3 3.7 %rows.1 = bf16[8,288,128]{2,1,0:T(8,128)(2,1)} custom-call(s32[1]{0:T(128)} %bitcast.feat_ref, s32[32,192]{1,0:T(8,128)} %bitcast.25, f32[172,1024]{1,0:T(8,128)} %bitcast.22, s32[1,1024]{1,0:T(1,128)} %bitcast.33), custom_call_target="tpu_custom_call" | custom-call | flops 1000000000 | bytes 2000000 | tf_op jit(solution)/shard_map/rows/pallas_call | solution.py:371
  21.0 3.7 %all-to-all-start.1 = ((bf16[8,288,128]{2,1,0:T(8,128)(2,1)}), bf16[8,288,128]{2,1,0:T(8,128)(2,1)S(1)}, u32[]{:S(2)}, u32[]{:S(2)}) async-start(bf16[8,288,128]{2,1,0:T(8,128)(2,1)} %rows.1), calls=%async_computation.1 | async-start | bytes 1179648 | tf_op jit(solution)/shard_map/all_to_all | solution.py:378
  24.7 2.2 %pack.1 = (bf16[976,128]{1,0:T(8,128)(2,1)}, bf16[976,128]{1,0:T(8,128)(2,1)}, bf16[976,128]{1,0:T(8,128)(2,1)}, bf16[976,128]{1,0:T(8,128)(2,1)}) custom-call(s32[1]{0:T(128)} %bitcast.feat_ref, bf16[64,2048]{1,0:T(8,128)(2,1)} %bitcast.21, f32[3,43,700]{2,1,0:T(8,128)} %bitcast.19), custom_call_target="tpu_custom_call" | custom-call | flops 100000000 | bytes 1000000 | tf_op jit(solution)/shard_map/pack/pallas_call | solution.py:359
  26.9 0.1 collective-permute-start
  27.0 0.5 collective-permute-start.1
  27.5 1.4 %collective-permute-start.2 = (bf16[976,128]{1,0:T(8,128)(2,1)}, bf16[976,128]{1,0:T(8,128)(2,1)S(1)}, u32[]{:S(2)}, u32[]{:S(2)}) collective-permute-start(bf16[976,128]{1,0:T(8,128)(2,1)} %get-tuple-element.11), channel_id=1, source_target_pairs={{0,3},{1,0},{2,1},{3,2},{4,7},{5,4},{6,5},{7,6},{8,11},{9,8},{10,9... | collective-permute-start | bytes 749576 | tf_op jit(solution)/shard_map/ppermute | solution.py:367
  28.9 0.0 copy-done.3
  28.9 0.8 copy.34.ref_ref
  29.7 0.0 copy-done.5
  29.7 0.9 copy.35.time_ref
  30.6 0.6 slice.4.reft_ref
  31.2 3.6 %collective-permute-done.rest_1_ = bf16[976,128]{1,0:T(8,128)(2,1)S(1)} collective-permute-done((bf16[976,128]{1,0:T(8,128)(2,1)}, bf16[976,128]{1,0:T(8,128)(2,1)S(1)}, u32[]{:S(2)}, u32[]{:S(2)}) %collective-permute-start) | collective-permute-done | bytes 249888 | tf_op jit(solution)/shard_map/ppermute | solution.py:367
  34.8 1.4 %collective-permute-done.1.rest_2_ = bf16[976,128]{1,0:T(8,128)(2,1)S(1)} collective-permute-done((bf16[976,128]{1,0:T(8,128)(2,1)}, bf16[976,128]{1,0:T(8,128)(2,1)S(1)}, u32[]{:S(2)}, u32[]{:S(2)}) %collective-permute-start.1) | collective-permute-done | bytes 249888 | tf_op jit(solution)/shard_map/ppermute | solution.py:367
  36.2 2.8 %collective-permute-done.2.rest_3_ = bf16[976,128]{1,0:T(8,128)(2,1)S(1)} collective-permute-done((bf16[976,128]{1,0:T(8,128)(2,1)}, bf16[976,128]{1,0:T(8,128)(2,1)S(1)}, u32[]{:S(2)}, u32[]{:S(2)}) %collective-permute-start.2) | collective-permute-done | bytes 249888 | tf_op jit(solution)/shard_map/ppermute | solution.py:367
  39.0 2.1 %all-to-all-done.1.rows_ref = bf16[8,288,128]{2,1,0:T(8,128)(2,1)S(1)} async-done(((bf16[8,288,128]{2,1,0:T(8,128)(2,1)}), bf16[8,288,128]{2,1,0:T(8,128)(2,1)S(1)}, u32[]{:S(2)}, u32[]{:S(2)}) %all-to-all-start.1) | async-done | bytes 589856 | tf_op jit(solution)/shard_map/all_to_all | solution.py:378
  41.1 0.0 copy-done.9
  41.1 0.0 copy-done.10
  41.1 0.0 copy-done.11
  41.1 0.8 copy-done.1
  41.9 7.7 %messages.1 = (bf16[1536,256]{1,0:T(8,128)(2,1)}, bf16[32,208,128]{2,1,0:T(8,128)(2,1)}) custom-call(s32[1]{0:T(128)} %bitcast.feat_ref, bf16[8,288,128]{2,1,0:T(8,128)(2,1)} %copy-done.1, s32[512,12]{1,0:T(8,128)} %copy.34.ref_ref, s32[2,512]{1,0:T(2,128)} %slice.4.reft_ref, s32[512,1]{1,0:T(8,128)} %copy.35.time_ref, f32[1,100]{1,0:T(1,128)} %bitcast.28, ...), custom_call_target="tpu_custom_call" | custom-call | flops 4000000000 | bytes 4000000 | tf_op jit(solution)/shard_map/messages/pallas_call | solution.py:391
  49.6 0.0 copy-start.4
  49.6 0.0 copy-start.2
  49.6 4.5 %all-to-all-start.2 = ((bf16[32,208,128]{2,1,0:T(8,128)(2,1)}), bf16[32,208,128]{2,1,0:T(8,128)(2,1)S(1)}, u32[]{:S(2)}, u32[]{:S(2)}) async-start(bf16[32,208,128]{2,1,0:T(8,128)(2,1)} %get-tuple-element.13), calls=%async_computation.2 | async-start | bytes 3407872 | tf_op jit(solution)/shard_map/all_to_all | solution.py:406
  54.1 0.0 copy-done.7
  54.1 0.6 pad.7.freq_ref
  54.7 0.0 copy-done.8
  54.7 0.6 pad.8.phase_ref
  55.4 0.0 copy-done.6
  55.4 0.7 copy.39
  56.1 0.0 copy-done.4
  56.1 0.8 copy.37.gap_ref
  56.9 0.0 copy-done.2
  56.9 0.8 copy.38.wm_ref
  57.7 1.6 %dynamic-slice_bitcast_fusion.own_ref = f32[43,1024]{1,0:T(8,128)} fusion(f32[1024,172]{0,1:T(8,128)} %param.19, s32[]{:T(128)S(6)} %select_n.3), kind=kLoop, calls=%fused_computation | loop fusion | bytes 352260 | tf_op jit(solution)/shard_map/dynamic_slice | solution.py:466
  59.4 3.8 %state.1.state_ref = f32[4,43,1024]{2,1,0:T(8,128)} custom-call(f32[172,1024]{1,0:T(8,128)} %bitcast.23, f32[3,43,700]{2,1,0:T(8,128)} %bitcast.20, f32[3,43,172]{2,1,0:T(8,128)} %bitcast.32, f32[43,4]{1,0:T(8,128)} %bitcast.26), custom_call_target="tpu_custom_call" | custom-call | flops 3000000000 | bytes 3000000 | tf_op jit(solution)/shard_map/state/pallas_call | solution.py:380
  63.1 0.1 reduce.1
  63.2 0.7 reshape_reshape.3.ids_ref
  63.9 30.2 %embed.1 = bf16[512,172]{1,0:T(8,128)(2,1)} custom-call(bf16[1536,256]{1,0:T(8,128)(2,1)} %get-tuple-element.12.table_ref, s32[512,12]{1,0:T(8,128)} %copy.34.ref_ref, s32[512,10]{1,0:T(8,128)} %copy.37.gap_ref, f32[1,256]{1,0:T(1,128)} %pad.7.freq_ref, f32[1,256]{1,0:T(1,128)} %pad.8.phase_ref, bf16[272,272]{1,0:T(8,128)(2,1)} %wq_ref.1, ...), custom_call_target="tpu_custom_call" | custom-call | flops 20000000000 | bytes 4000000 | tf_op jit(solution)/shard_map/embed/pallas_call | solution.py:412
  94.2 1.7 %copy.40 = bf16[512,172]{0,1:T(8,128)(2,1)} copy(bf16[512,172]{1,0:T(8,128)(2,1)} %embed.1) | data formatting | bytes 352256
  95.9 0.0 all-to-all-done.2.recv_ref
  95.9 1.2 %copy-done = bf16[32,208,128]{2,1,0:T(8,128)(2,1)} copy-done((bf16[32,208,128]{2,1,0:T(8,128)(2,1)}, bf16[32,208,128]{2,1,0:T(8,128)(2,1)S(1)}, u32[]{:S(2)}) %copy-start) | copy-done | bytes 1703960
  97.1 8.4 %update.1 = f32[43,1024]{1,0:T(8,128)} custom-call(bf16[32,208,128]{2,1,0:T(8,128)(2,1)} %copy-done, s32[8,1,768]{2,1,0:T(1,128)} %reshape_reshape.3.ids_ref, f32[4,43,1024]{2,1,0:T(8,128)} %state.1.state_ref, f32[43,1024]{1,0:T(8,128)} %dynamic-slice_bitcast_fusion.own_ref), custom_call_target="tpu_custom_call" | custom-call | flops 4000000000 | bytes 4000000 | tf_op jit(solution)/shard_map/update/pallas_call | solution.py:456
  (11 shorter events, 0.0 us)
Async XLA Ops:
  2.1 14.6 %all-to-all-start = ((s32[32,1,192]{2,1,0:T(1,128)}), s32[32,1,192]{2,1,0:T(1,128)S(1)}, u32[]{:S(2)}, u32[]{:S(2)}) async-start(s32[32,1,192]{2,1,0:T(1,128)} %reshape.34), calls=%async_computation | async-start | bytes 65536 | tf_op jit(solution)/shard_map/all_to_all | solution.py:347
  21.0 7.9 %copy-start.3 = (s32[512,12]{0,1:T(8,128)S(1)}, s32[512,12]{0,1:T(8,128)}, u32[]{:S(2)}) copy-start(s32[512,12]{0,1:T(8,128)} %param.24) | copy-start | bytes 73732
  21.0 8.7 %copy-start.5 = (s32[512]{0:T(512)S(1)}, s32[512]{0:T(512)}, u32[]{:S(2)}) copy-start(s32[512]{0:T(512)} %param.21) | copy-start | bytes 6148
  21.0 20.1 %all-to-all-start.1 = ((bf16[8,288,128]{2,1,0:T(8,128)(2,1)}), bf16[8,288,128]{2,1,0:T(8,128)(2,1)S(1)}, u32[]{:S(2)}, u32[]{:S(2)}) async-start(bf16[8,288,128]{2,1,0:T(8,128)(2,1)} %rows.1), calls=%async_computation.1 | async-start | bytes 1179648 | tf_op jit(solution)/shard_map/all_to_all | solution.py:378
  26.9 7.9 %collective-permute-start = (bf16[976,128]{1,0:T(8,128)(2,1)}, bf16[976,128]{1,0:T(8,128)(2,1)S(1)}, u32[]{:S(2)}, u32[]{:S(2)}) collective-permute-start(bf16[976,128]{1,0:T(8,128)(2,1)} %get-tuple-element.9), channel_id=1, source_target_pairs={{0,1},{1,2},{2,3},{3,0},{4,5},{5,6},{6,7},{7,4},{8,9},{9,10},{10,1... | collective-permute-start | bytes 749576 | tf_op jit(solution)/shard_map/ppermute | solution.py:367
  27.0 9.1 %collective-permute-start.1 = (bf16[976,128]{1,0:T(8,128)(2,1)}, bf16[976,128]{1,0:T(8,128)(2,1)S(1)}, u32[]{:S(2)}, u32[]{:S(2)}) collective-permute-start(bf16[976,128]{1,0:T(8,128)(2,1)} %get-tuple-element.10), channel_id=1, source_target_pairs={{0,2},{1,3},{2,0},{3,1},{4,6},{5,7},{6,4},{7,5},{8,10},{9,11},{10,... | collective-permute-start | bytes 749576 | tf_op jit(solution)/shard_map/ppermute | solution.py:367
  27.5 11.4 %collective-permute-start.2 = (bf16[976,128]{1,0:T(8,128)(2,1)}, bf16[976,128]{1,0:T(8,128)(2,1)S(1)}, u32[]{:S(2)}, u32[]{:S(2)}) collective-permute-start(bf16[976,128]{1,0:T(8,128)(2,1)} %get-tuple-element.11), channel_id=1, source_target_pairs={{0,3},{1,0},{2,1},{3,2},{4,7},{5,4},{6,5},{7,6},{8,11},{9,8},{10,9... | collective-permute-start | bytes 749576 | tf_op jit(solution)/shard_map/ppermute | solution.py:367
  34.8 6.3 %copy-start.9 = (bf16[976,128]{1,0:T(8,128)(2,1)}, bf16[976,128]{1,0:T(8,128)(2,1)S(1)}, u32[]{:S(2)}) copy-start(bf16[976,128]{1,0:T(8,128)(2,1)S(1)} %collective-permute-done.rest_1_) | copy-start | bytes 749572
  36.2 4.9 %copy-start.10 = (bf16[976,128]{1,0:T(8,128)(2,1)}, bf16[976,128]{1,0:T(8,128)(2,1)S(1)}, u32[]{:S(2)}) copy-start(bf16[976,128]{1,0:T(8,128)(2,1)S(1)} %collective-permute-done.1.rest_2_) | copy-start | bytes 749572
  39.0 2.1 %copy-start.11 = (bf16[976,128]{1,0:T(8,128)(2,1)}, bf16[976,128]{1,0:T(8,128)(2,1)S(1)}, u32[]{:S(2)}) copy-start(bf16[976,128]{1,0:T(8,128)(2,1)S(1)} %collective-permute-done.2.rest_3_) | copy-start | bytes 749572
  41.1 0.8 copy-start.1
  49.5 4.5 %copy-start.7 = (f32[100]{0:T(128)S(1)}, f32[100]{0:T(128)}, u32[]{:S(2)}) copy-start(f32[100]{0:T(128)} %param.26) | copy-start | bytes 1204
  49.5 5.2 %copy-start.8 = (f32[100]{0:T(128)S(1)}, f32[100]{0:T(128)}, u32[]{:S(2)}) copy-start(f32[100]{0:T(128)} %param.27) | copy-start | bytes 1204
  49.5 5.8 %copy-start.6 = (f32[4,43]{1,0:T(4,128)S(1)}, f32[4,43]{1,0:T(4,128)}, u32[]{:S(2)}) copy-start(f32[4,43]{1,0:T(4,128)} %param.37) | copy-start | bytes 2068
  49.6 6.5 %copy-start.4 = (s32[512,10]{0,1:T(8,128)S(1)}, s32[512,10]{0,1:T(8,128)}, u32[]{:S(2)}) copy-start(s32[512,10]{0,1:T(8,128)} %param.22) | copy-start | bytes 61444
  49.6 7.3 %copy-start.2 = (bf16[444,172]{0,1:T(8,128)(2,1)S(1)}, bf16[444,172]{0,1:T(8,128)(2,1)}, u32[]{:S(2)}) copy-start(bf16[444,172]{0,1:T(8,128)(2,1)} %param.31) | copy-start | bytes 458212
  49.6 46.3 %all-to-all-start.2 = ((bf16[32,208,128]{2,1,0:T(8,128)(2,1)}), bf16[32,208,128]{2,1,0:T(8,128)(2,1)S(1)}, u32[]{:S(2)}, u32[]{:S(2)}) async-start(bf16[32,208,128]{2,1,0:T(8,128)(2,1)} %get-tuple-element.13), calls=%async_computation.2 | async-start | bytes 3407872 | tf_op jit(solution)/shard_map/all_to_all | solution.py:406
  95.9 1.2 %copy-start = (bf16[32,208,128]{2,1,0:T(8,128)(2,1)}, bf16[32,208,128]{2,1,0:T(8,128)(2,1)S(1)}, u32[]{:S(2)}) copy-start(bf16[32,208,128]{2,1,0:T(8,128)(2,1)S(1)} %all-to-all-done.2.recv_ref) | copy-start | bytes 5111812

commit v2 on v1

v2 whole, which is shorter than its diff:
```python
import functools
import math

import jax
import jax.numpy as jnp
from jax import lax
from jax.experimental import pallas as pl
from jax.experimental.pallas import tpu as pltpu
from jax.sharding import PartitionSpec as P


HEADS = 2
LANES = 128
HALF = 64
GROUP = 3
EVENT_TILE = 128
STAMP_SHIFT = 6
HIT_BASE = 32.0
SPLIT = 2

bf16 = jnp.bfloat16
f32 = jnp.float32
exact = lax.Precision.HIGHEST


def rounded(count, step):
    return -(-count // step) * step


def cosine(x):
    turns = jnp.floor(x * (1.0 / math.pi) + 0.5)
    r = x - turns * 3.140625
    r = r - turns * 9.67502593994140625e-4
    r = r - turns * 1.509957990978376432e-7
    half = turns * 0.5
    sign = 1.0 - 4.0 * (half - jnp.floor(half))
    s = r * r
    poly = 1.0 / 479001600.0
    for coef in (-1.0 / 3628800.0, 1.0 / 40320.0, -1.0 / 720.0, 1.0 / 24.0, -0.5, 1.0):
        poly = poly * s + coef
    return poly * sign


def mm(a, b):
    return jnp.dot(a, b, preferred_element_type=f32)


def mm_nt(a, b):
    return lax.dot_general(a, b, (((1,), (1,)), ((), ())), preferred_element_type=f32)


def hot(mask):
    return jnp.where(mask, 1.0, 0.0).astype(bf16)


def iota(shape, axis):
    return lax.broadcasted_iota(jnp.int32, shape, axis)


PART, TIME_AT, EDGE_AT, COLS = 256, 256, 384, 640
PIECES = COLS // LANES
SPARE_ROWS = 16


def pack_kernel(mem, time, feat, feat_ref, edge_ref, w_ref, memory_ref, stamp_ref, table_ref, *out_refs):
    rows = memory_ref.shape[1]
    stamps = stamp_ref[...]
    high = lax.shift_right_logical(stamps, STAMP_SHIFT)
    low = stamps - lax.shift_left(high, STAMP_SHIFT)
    tail = jnp.concatenate([high, low, jnp.zeros((table_ref.shape[0] - mem - 2, rows), jnp.int32)], 0).astype(f32)
    table_ref[...] = jnp.concatenate([memory_ref[...], tail], 0).astype(bf16)
    own, events = edge_ref.shape
    events = events // feat
    gates, width, raw = w_ref.shape
    lines = jnp.concatenate([w_ref[g] for g in range(gates)], 0)
    lines = jnp.concatenate([lines, jnp.zeros((LANES + SPARE_ROWS - gates * width, raw), f32)], 0)
    height = lines.shape[0]
    fill = lambda count: jnp.zeros((height, count), f32)
    lines = jnp.concatenate(
        [
            lines[:, mem : 2 * mem],
            fill(PART - mem),
            lines[:, 2 * mem : 2 * mem + time],
            fill(LANES - time),
            lines[:, 2 * mem + time :],
        ],
        1,
    ).astype(bf16)
    edge_rows = own * events // LANES
    for k, out_ref in enumerate(out_refs):
        dest = lax.rem(feat_ref[0] + k, feat)
        block = edge_ref[:, pl.ds(pl.multiple_of(dest * events, LANES), events)]
        for c in range(events // LANES):
            out_ref[c * own : (c + 1) * own, :] = block[:, c * LANES : (c + 1) * LANES]
        for c in range(PIECES):
            at = edge_rows + c * height
            out_ref[at : at + height, :] = lines[:, c * LANES : (c + 1) * LANES]


def places_of(slot, nodes, per_owner):
    full = per_owner // LANES * LANES
    owner = jnp.zeros_like(slot)
    for n in range(1, nodes):
        owner = owner + (slot >= n * per_owner).astype(jnp.int32)
    within = slot - owner * per_owner
    piece = lax.shift_right_logical(within, 7)
    return jnp.where(
        within < full,
        (piece * nodes + owner) * LANES + within - piece * LANES,
        full * nodes + owner * HALF + within - full,
    )


def swapped(x):
    return pltpu.roll(x, HALF, 1)


def left(shape):
    return iota(shape, 1) < HALF


def split_pair(tile):
    top, low = tile[: tile.shape[0] // 2], tile[tile.shape[0] // 2 :]
    side = left(top.shape)
    return jnp.where(side, top, swapped(low)), jnp.where(side, swapped(top), low)


def join_pair(first, second):
    side = left(first.shape)
    return jnp.concatenate([jnp.where(side, first, swapped(second)), jnp.where(side, swapped(first), second)], 0)


def rows_kernel(full, ids_ref, table_ref, out_ref):
    nodes = out_ref.shape[0]
    per_owner = ids_ref.shape[1]
    rest = per_owner - full * LANES
    height, rows = table_ref.shape
    lines = [ids_ref[n : n + 1, :] for n in range(nodes)]
    ids = [lines[n][:, c * LANES : (c + 1) * LANES] for c in range(full) for n in range(nodes)]
    if rest:
        last = [line[:, full * LANES :] for line in lines]
        if rest < HALF:
            last = [jnp.concatenate([x, jnp.full((1, HALF - rest), -1, jnp.int32)], 1) for x in last]
        ids += [jnp.concatenate(last[n : n + 2], 1) for n in range(0, nodes, 2)]
    ids = jnp.concatenate(ids, 1)
    picked = mm(table_ref[...], hot(iota((rows, ids.shape[1]), 0) == ids))
    for c in range(full):
        for n in range(nodes):
            at = (c * nodes + n) * LANES
            out_ref[n, c * height : (c + 1) * height, :] = picked[:, at : at + LANES].astype(bf16)
    if rest:
        room = out_ref.shape[1] - full * height
        for n in range(0, nodes, 2):
            at = full * nodes * LANES + n * HALF
            for i, piece in enumerate(split_pair(picked[:, at : at + LANES])):
                if room > height // 2:
                    piece = jnp.concatenate([piece, jnp.zeros((room - height // 2, LANES), f32)], 0)
                out_ref[n + i, full * height :, :] = piece.astype(bf16)


def message_kernel(mem, per_owner, full, feat, own, feat_ref, rows_ref, slot_ref, time_ref, freq_ref, phase_ref, *rest_refs):
    pack_refs = rest_refs[:feat]
    table_out, out_ref, table_ref, w_ref, edge_ref, sem = rest_refs[feat:]
    nodes = rows_ref.shape[0]
    slots = table_ref.shape[1]
    events = slot_ref.shape[1]
    time = freq_ref.shape[0]
    rest = per_owner - full * LANES
    height = rounded(mem + 2, 16)
    source_of = [lax.rem(feat_ref[0] + feat - k, feat) for k in range(feat)]
    table_ref[height:, :] = jnp.zeros((table_ref.shape[0] - height, slots), bf16)
    for c in range(full):
        for n in range(nodes):
            at = (c * nodes + n) * LANES
            table_ref[0:height, at : at + LANES] = rows_ref[n, c * height : (c + 1) * height, :]
    if rest:
        for n in range(0, nodes, 2):
            at = full * nodes * LANES + n * HALF
            pair = [rows_ref[n + i, full * height :, :].astype(f32)[: height // 2] for i in range(2)]
            table_ref[0:height, at : at + LANES] = join_pair(*pair).astype(bf16)
    keep = pltpu.make_async_copy(table_ref, table_out, sem)
    keep.start()
    edge_rows = own * events // LANES
    tall = LANES + SPARE_ROWS
    for c in range(PIECES):
        spare = []
        for k in range(feat):
            at = edge_rows + c * tall
            w_ref[k * LANES : (k + 1) * LANES, c * LANES : (c + 1) * LANES] = pack_refs[k][at : at + LANES, :]
            spare.append(pack_refs[k][at + LANES : at + tall, :].astype(f32)[0:1])
        spare.append(jnp.zeros((SPARE_ROWS - feat, LANES), f32))
        w_ref[feat * LANES :, c * LANES : (c + 1) * LANES] = jnp.concatenate(spare, 0).astype(bf16)
    for k in range(feat):
        at = pl.multiple_of(source_of[k] * own, own)
        for c in range(events // LANES):
            edge_ref[pl.ds(at, own), c * LANES : (c + 1) * LANES] = pack_refs[k][c * own : (c + 1) * own, :]
    table = table_ref[0:height, :]
    slot_of = iota((slots, events), 0)
    place = places_of(slot_ref[0:2, :], nodes, per_owner)
    hots = [hot(slot_of == place[i : i + 1, :]) for i in range(2)]
    found = [mm(table, h) for h in hots]
    freq = freq_ref[...]
    phase = phase_ref[...]
    by_edge = mm(w_ref[:, EDGE_AT:COLS], edge_ref[...])
    height_all = w_ref.shape[0]
    ones = iota((height_all, events), 0) == feat * LANES + feat
    sums = None
    for i in range(2):
        stamps = found[i][mem : mem + 1, :] * float(1 << STAMP_SHIFT) + found[i][mem + 1 : mem + 2, :]
        code = cosine(freq * (time_ref[...].astype(f32) - stamps) + phase).astype(bf16)
        sent = mm(w_ref[:, 0:height], found[1 - i].astype(bf16)) + mm(w_ref[:, TIME_AT : TIME_AT + time], code) + by_edge
        part = mm_nt(jnp.where(ones, 1.0, sent).astype(bf16), hots[i])
        sums = part if sums is None else sums + part
    extra = sums[feat * LANES :, :]
    hits = extra[feat : feat + 1, :]
    high = jnp.floor(hits * (1.0 / HIT_BASE))
    low = hits - high * HIT_BASE
    row_id = iota((GROUP, LANES), 0)
    folded = full * LANES + (HALF if rest else 0)
    blank = jnp.zeros((out_ref.shape[1] - folded - GROUP * (full + (1 if rest else 0)), LANES), f32)

    def tail(k, at):
        cut = slice(at, at + LANES)
        return jnp.where(
            row_id == 0, extra[k : k + 1, cut], jnp.where(row_id == 1, high[:, cut], jnp.where(row_id == 2, low[:, cut], 0.0))
        )

    for k in range(feat):
        block = sums[k * LANES : (k + 1) * LANES, :]
        for n in range(0, nodes, 2):
            tails = [[], []]
            for c in range(full):
                for i in range(2):
                    at = (c * nodes + n + i) * LANES
                    out_ref[(n + i) * feat + source_of[k], c * LANES : (c + 1) * LANES, :] = block[:, at : at + LANES].astype(bf16)
                    tails[i].append(tail(k, at))
            if rest:
                at = full * nodes * LANES + n * HALF
                ends = tail(k, at)
                for i, piece in enumerate(split_pair(block[:, at : at + LANES])):
                    out_ref[(n + i) * feat + source_of[k], full * LANES : full * LANES + HALF, :] = piece.astype(bf16)
                    tails[i].append(swapped(ends) if i else ends)
            for i in range(2):
                pieces = tails[i] + ([blank] if blank.shape[0] else [])
                out_ref[(n + i) * feat + source_of[k], folded:, :] = jnp.concatenate(pieces, 0).astype(bf16)
    keep.wait()


def embed_kernel(mem, nodes, per_owner, table_ref, ref_ref, gap_ref, freq_ref, phase_ref, wq_ref, wk_ref, wv_ref, wm_ref, bm_ref, wo_ref, bo_ref, out_ref, hot_ref, key_ref, prod_ref):
    tile, columns = ref_ref.shape
    nbrs = columns - 2
    slots = table_ref.shape[1]
    att = wq_ref.shape[0]
    head = att // HEADS
    slot_of = iota((tile, slots), 1)
    place = places_of(ref_ref[...], nodes, per_owner)
    hot_ref[0:tile, :] = hot(place[:, 0:1] == slot_of)
    for k in range(nbrs):
        hot_ref[(k + 1) * tile : (k + 2) * tile, :] = hot(place[:, 2 + k : 3 + k] == slot_of)
    fetched = mm_nt(hot_ref[...], table_ref[...])
    freq = freq_ref[...]
    phase = phase_ref[...]
    kept = iota((tile, LANES), 1) < mem - LANES
    for k in range(nbrs + 1):
        at = k * tile
        if k == 0:
            angle = jnp.broadcast_to(phase, (tile, 2 * LANES))
        else:
            angle = gap_ref[:, k - 1 : k].astype(f32) * freq + phase
        wave = cosine(angle)
        key_ref[at : at + tile, 0:LANES] = fetched[at : at + tile, :LANES].astype(bf16)
        key_ref[at : at + tile, LANES : 2 * LANES] = jnp.where(kept, fetched[at : at + tile, LANES:], wave[:, :LANES]).astype(bf16)
        key_ref[at : at + tile, 2 * LANES : att] = wave[:, LANES : att - LANES].astype(bf16)
    query = mm(key_ref[0:tile, :], wq_ref[...]) * (1.0 / math.sqrt(head))
    keys = mm(key_ref[tile:, :], wk_ref[...])
    values = mm(key_ref[tile:, :], wv_ref[...])
    for k in range(nbrs):
        prod_ref[k * tile : (k + 1) * tile, :] = keys[k * tile : (k + 1) * tile, :] * query
    prod = prod_ref[...]
    gather = hot((iota((att, LANES), 0) >= head).astype(jnp.int32) == (iota((att, LANES), 1) & 1))
    high = prod.astype(bf16)
    scores = mm(high, gather) + mm((prod - high.astype(f32)).astype(bf16), gather)
    parts = [scores[k * tile : (k + 1) * tile, :] for k in range(nbrs)]
    top = functools.reduce(jnp.maximum, parts)
    parts = [jnp.exp(s - top) for s in parts]
    scale = 1.0 / functools.reduce(jnp.add, parts)
    spread = hot(
        ((iota((LANES, att), 1) >= head).astype(jnp.int32) == (iota((LANES, att), 0) & 1)) & (iota((LANES, att), 0) < 4)
    )
    upper = iota((tile, LANES), 1) < 2
    attended = jnp.zeros((tile, att), f32)
    for k in range(nbrs):
        w = parts[k] * scale
        w_high = w.astype(bf16).astype(f32)
        w = jnp.where(upper, w_high, w - w_high).astype(bf16)
        attended = attended + mm(w, spread) * values[k * tile : (k + 1) * tile, :]
    merged = mm(attended.astype(bf16), wm_ref[0:att, :]) + mm(key_ref[0:tile, 0:mem], wm_ref[att : att + mem, :])
    hidden = jnp.maximum(merged + bm_ref[...], 0.0).astype(bf16)
    out_ref[...] = (mm(hidden, wo_ref[...]) + bo_ref[...]).astype(bf16)


def state_kernel(memory_ref, w_in_ref, w_hid_ref, bias_ref, out_ref):
    memory = memory_ref[...]
    mem = memory.shape[0]
    bias = bias_ref[...]

    def part(w, g):
        out_ref[g] = jnp.dot(w, memory, precision=exact, preferred_element_type=f32) + bias[:, g : g + 1]

    part(w_in_ref[0, :, 0:mem] + w_hid_ref[0], 0)
    part(w_in_ref[1, :, 0:mem] + w_hid_ref[1], 1)
    part(w_in_ref[2, :, 0:mem], 2)
    part(w_hid_ref[2], 3)


def update_kernel(full, rest, feat, feat_ref, recv_ref, ids_ref, state_hbm, own_hbm, out_ref, acc_ref, state_ref, own_ref, sem):
    rows = acc_ref.shape[1]
    width = own_ref.shape[0]
    loads = [pltpu.make_async_copy(state_hbm, state_ref, sem.at[0]), pltpu.make_async_copy(own_hbm, own_ref, sem.at[1])]
    for load in loads:
        load.start()
    acc_ref[...] = jnp.zeros_like(acc_ref)
    folded = full * LANES + (HALF if rest else 0)
    source_of = [lax.rem(feat_ref[0] + feat - k, feat) for k in range(feat)]

    def step(i, carry):
        main, side = [], []
        tails = [recv_ref[i * feat + source_of[b], folded:, :].astype(f32) for b in range(feat)]
        for c in range(full):
            for b in range(feat):
                main.append(recv_ref[i * feat + source_of[b], c * LANES : (c + 1) * LANES, :])
                side.append(tails[b][c * GROUP : (c + 1) * GROUP])
        if rest:
            for b in range(0, feat, 2):
                pair = [recv_ref[i * feat + source_of[b + j], full * LANES : folded, :].astype(f32) for j in range(2)]
                main.append(join_pair(*pair).astype(bf16))
                ends = [tails[b + j][full * GROUP : (full + 1) * GROUP] for j in range(2)]
                side.append(jnp.where(left(ends[0].shape), ends[0], swapped(ends[1])))
        side = jnp.concatenate(side, 1)
        side = jnp.concatenate([side, jnp.zeros((16 - GROUP, side.shape[1]), f32)], 0).astype(bf16)
        data = jnp.concatenate([jnp.concatenate(main, 1), side], 0)
        ids = ids_ref[i]
        data = jnp.concatenate([data * hot((ids >= h * rows) & (ids < (h + 1) * rows)) for h in range(SPLIT)], 0)
        acc_ref[...] += mm_nt(data, hot(iota((rows, ids.shape[1]), 0) == ids % rows))
        return carry

    steps = recv_ref.shape[0] // feat
    lax.fori_loop(0, steps, step, 0, unroll=steps <= 8)
    for load in loads:
        load.wait()
    height = acc_ref.shape[0] // SPLIT
    acc = jnp.concatenate([acc_ref[h * height : (h + 1) * height, :] for h in range(SPLIT)], 1)
    at = 3 * width
    hits = acc[at : at + 1, :] * HIT_BASE + acc[at + 1 : at + 2, :]
    scale = 1.0 / jnp.maximum(hits, 1.0)
    own = own_ref[...]
    reset = jax.nn.sigmoid(acc[0:width, :] * scale + state_ref[0])
    update = jax.nn.sigmoid(acc[width : 2 * width, :] * scale + state_ref[1])
    fresh = jnp.tanh(acc[2 * width : 3 * width, :] * scale + state_ref[2] + reset * state_ref[3])
    out_ref[...] = jnp.where(hits > 0.0, (1.0 - update) * fresh + update * own, own)


def modest():
    return pltpu.CompilerParams(vmem_limit_bytes=40 << 20)


def on_chip(shape, kind):
    return pltpu.VMEM(shape, kind)


def hold(x):
    return pltpu.with_memory_space_constraint(x, pltpu.VMEM)


def off_chip(x):
    return pltpu.with_memory_space_constraint(x, pltpu.HBM)


def cost(flops, moved):
    return pl.CostEstimate(flops=int(flops), transcendentals=0, bytes_accessed=int(moved))


def per_device(
    memory,
    last_update,
    ev_time,
    nbr_gap,
    slot_rows,
    slot_ref,
    edge_feat,
    frequency,
    phase_shift,
    w_query,
    w_key,
    w_value,
    w_merge,
    b_merge,
    w_out,
    b_out,
    w_input,
    w_hidden,
    gru_bias,
):
    nodes = lax.axis_size("node")
    feat = lax.axis_size("feat")
    blocks = nodes * feat
    rows, mem = memory.shape
    slots = slot_rows.shape[1]
    per_owner = slots // nodes
    events, columns = slot_ref.shape
    time = frequency.shape[0]
    att = w_query.shape[0]
    emb = w_out.shape[1]
    width = w_hidden.shape[2]
    everyone = ("node", "feat")

    asked = slot_rows.reshape(nodes, 1, per_owner)
    asked = lax.all_to_all(asked, "node", split_axis=0, concat_axis=0, tiled=True).reshape(nodes, per_owner)

    here = lax.axis_index("feat").astype(jnp.int32)
    here_line = here.reshape(1)
    memory_t = memory.T
    w_input_t = jnp.swapaxes(w_input, 1, 2)
    w_hidden_t = jnp.swapaxes(w_hidden, 1, 2)
    smem = pl.BlockSpec(memory_space=pltpu.SMEM)
    vmem = pl.BlockSpec(memory_space=pltpu.VMEM)
    hbm = pl.BlockSpec(memory_space=pltpu.HBM)
    auto = pl.BlockSpec()

    own = edge_feat.shape[1]
    height = own * events // LANES + PIECES * (LANES + SPARE_ROWS)
    high_rows = rounded(mem + 2, 16)
    table, *packed = pl.pallas_call(
        functools.partial(pack_kernel, mem, time, feat),
        in_specs=[smem, auto, auto, auto, auto],
        out_shape=[jax.ShapeDtypeStruct((high_rows, rows), bf16)]
        + [jax.ShapeDtypeStruct((height, LANES), bf16)] * feat,
        cost_estimate=cost(1e8, 1e6),
        compiler_params=modest(),
        name="pack",
    )(here_line, off_chip(edge_feat.T), off_chip(w_input_t), off_chip(memory_t), last_update.reshape(1, rows))
    asked, table, *packed = lax.optimization_barrier((asked, table, *packed))
    turn = lambda k: [(i, (i + k) % feat) for i in range(feat)]
    packed = [packed[0]] + [lax.ppermute(packed[k], "feat", turn(k)) for k in range(1, feat)]

    full = per_owner // LANES
    rest = per_owner - full * LANES
    assert rest <= HALF and nodes % 2 == 0
    room = full * high_rows + (rounded(high_rows // 2, 8) if rest else 0)
    found = pl.pallas_call(
        functools.partial(rows_kernel, full),
        out_shape=on_chip((nodes, room, LANES), bf16),
        in_specs=[vmem, vmem],
        out_specs=vmem,
        cost_estimate=cost(1e9, 2e6),
        compiler_params=modest(),
        name="rows",
    )(asked, table)
    found = lax.all_to_all(found, "node", split_axis=0, concat_axis=0, tiled=True)

    state = pl.pallas_call(
        state_kernel,
        out_shape=pltpu.HBM((4, width, rows), f32),
        cost_estimate=cost(3e9, 3e6),
        compiler_params=modest(),
        name="state",
    )(off_chip(memory_t), off_chip(w_input_t), off_chip(w_hidden_t), gru_bias.T)

    places = nodes * (full * LANES + (HALF if rest else 0))
    freq_line = frequency.reshape(1, time)
    phase_line = phase_shift.reshape(1, time)
    shift = mem - LANES
    spread = ((0, 0), (shift, 2 * LANES - shift - time))
    freq_wide, phase_wide = jnp.pad(freq_line, spread), jnp.pad(phase_line, spread)
    own_cols = lax.dynamic_slice_in_dim(memory_t, here * width, width, 0)
    asked = jnp.stack([asked] + [lax.ppermute(asked, "feat", turn(k)) for k in range(1, feat)], 1)
    ids = [asked[:, :, c * LANES : (c + 1) * LANES].reshape(nodes, 1, feat * LANES) for c in range(full)]
    if rest:
        last = jnp.pad(asked[:, :, full * LANES :], ((0, 0), (0, 0), (0, HALF - rest)), constant_values=-1)
        ids.append(last.reshape(nodes, 1, feat * HALF))
    ids = jnp.concatenate(ids, 2)
    found, freq_wide, phase_wide, own_cols, state, ids = lax.optimization_barrier(
        (found, freq_wide, phase_wide, own_cols, state, ids)
    )
    ends = full + (1 if rest else 0)
    depth = full * LANES + (HALF if rest else 0) + rounded(GROUP * ends, 8)
    fetched, sums = pl.pallas_call(
        functools.partial(message_kernel, mem, per_owner, full, feat, own),
        in_specs=[smem] + [vmem] * (5 + feat),
        out_specs=(hbm, vmem),
        out_shape=(
            pltpu.HBM((2 * LANES, places), bf16),
            on_chip((blocks, depth, LANES), bf16),
        ),
        scratch_shapes=[
            pltpu.VMEM((2 * LANES, places), bf16),
            pltpu.VMEM((feat * LANES + SPARE_ROWS, COLS), bf16),
            pltpu.VMEM((feat * own, events), bf16),
            pltpu.SemaphoreType.DMA,
        ],
        cost_estimate=cost(4e9, 4e6),
        compiler_params=modest(),
        name="messages",
    )(
        here_line,
        hold(found),
        slot_ref.T,
        ev_time.reshape(1, events),
        frequency.reshape(time, 1),
        phase_shift.reshape(time, 1),
        *[hold(x) for x in packed],
    )
    sums = lax.all_to_all(sums, everyone, split_axis=0, concat_axis=0, tiled=True)

    nbrs = columns - 2
    whole = lambda shape: pl.BlockSpec(shape, lambda i: (0,) * len(shape))
    embedding = pl.pallas_call(
        functools.partial(embed_kernel, mem, nodes, per_owner),
        grid=(events // EVENT_TILE,),
        in_specs=[
            whole((2 * LANES, places)),
            pl.BlockSpec((EVENT_TILE, columns), lambda i: (i, 0)),
            pl.BlockSpec((EVENT_TILE, nbrs), lambda i: (i, 0)),
            whole((1, 2 * LANES)),
            whole((1, 2 * LANES)),
            whole((att, att)),
            whole((att, att)),
            whole((att, att)),
            whole((att + mem, emb)),
            whole((1, emb)),
            whole((emb, emb)),
            whole((1, emb)),
        ],
        out_specs=pl.BlockSpec((EVENT_TILE, emb), lambda i: (i, 0)),
        out_shape=jax.ShapeDtypeStruct((events, emb), bf16),
        scratch_shapes=[
            pltpu.VMEM(((nbrs + 1) * EVENT_TILE, places), bf16),
            pltpu.VMEM(((nbrs + 1) * EVENT_TILE, att), bf16),
            pltpu.VMEM((nbrs * EVENT_TILE, att), f32),
        ],
        cost_estimate=cost(2e10, 4e6),
        compiler_params=modest(),
        name="embed",
    )(
        off_chip(fetched),
        slot_ref,
        nbr_gap,
        freq_wide,
        phase_wide,
        off_chip(w_query),
        off_chip(w_key),
        off_chip(w_value),
        w_merge,
        b_merge.reshape(1, emb),
        off_chip(w_out),
        b_out.reshape(1, emb),
    )

    new_memory = pl.pallas_call(
        functools.partial(update_kernel, full, rest, feat),
        in_specs=[smem, vmem, vmem, hbm, hbm],
        out_specs=vmem,
        out_shape=jax.ShapeDtypeStruct((width, rows), f32),
        scratch_shapes=[
            pltpu.VMEM((SPLIT * (LANES + 16), rows // SPLIT), f32),
            pltpu.VMEM((4, width, rows), f32),
            pltpu.VMEM((width, rows), f32),
            pltpu.SemaphoreType.DMA((2,)),
        ],
        cost_estimate=cost(4e9, 4e6),
        compiler_params=modest(),
        name="update",
    )(here_line, hold(sums), ids, off_chip(state), off_chip(own_cols))
    return (embedding, new_memory.T)


def solution(mesh):
    return jax.shard_map(
        per_device,
        mesh=mesh,
        in_specs=(
            P("node", None),
            P("node"),
            P(("node", "feat")),
            P(("node", "feat"), None),
            P(("node", "feat"), None),
            P(("node", "feat"), None),
            P("node", "feat"),
            P(),
            P(),
            P(),
            P(),
            P(),
            P(),
            P(),
            P(),
            P(),
            P(None, None, "feat"),
            P(None, None, "feat"),
            P(None, "feat"),
        ),
        out_specs=(P(("node", "feat"), None), P("node", "feat")),
        check_vma=False,
    )
```

time: 106 us -> 93.8 us (0.88)
  Pallas kernels: 56.1 us -> 45.7 us
  local copies, waits for them, and re-layouts: 13.4 us -> 4.84 us
  starting transfers between devices: 17.4 us -> 21.1 us
  waiting for transfers between devices: 17.1 us -> 19.8 us
    pallas_call x5, Pallas kernels: 53.8 us -> 44.2 us  [the longest x1 29.7 us: per_device(): pl.pallas_call(functools.partial(embed_kernel, mem, nodes, per_owner), gr...]
    all_to_all x1, waiting for transfers between devices: 0.01 us -> 7.9 us  [per_device(): lax.all_to_all(sums, everyone, split_axis=0, concat_axis=0, tiled=True)]
    unnamed x30 -> x26, local copies, waits for them, and re-layouts: 7.64 us -> 2.04 us
    ppermute x3 -> x6, waiting for transfers between devices: 7.77 us -> 3.81 us  [the longest x3 3.8 us: per_device(): lax.ppermute(packed[k], 'feat', turn(k))]
    all_to_all x1, waiting for transfers between devices: 7.25 us -> 4.3 us  [per_device(): lax.all_to_all(asked, 'node', split_axis=0, concat_axis=0, tiled=True)]
    all_to_all x1, starting transfers between devices: 4.48 us -> 6.58 us  [per_device(): lax.all_to_all(sums, everyone, split_axis=0, concat_axis=0, tiled=True)]
    ppermute x3 -> x6, starting transfers between devices: 1.97 us -> 3.71 us  [the longest x3 1.98 us: per_device(): lax.ppermute(packed[k], 'feat', turn(k))]
    all_to_all x1, waiting for transfers between devices: 2.1 us -> 3.75 us  [per_device(): lax.all_to_all(found, 'node', split_axis=0, concat_axis=0, tiled=True)]
  transfers between devices with their start and end apart: 6 -> 9, of which waited for: 5 -> 5; matrix products, arithmetic and copies ran while one was open for 10% -> 4% of each run, Pallas kernels for 34% -> 38%
where the time goes in v2:
time: 93.8 us; the launch traced here: 93.2 us
  Pallas kernels  45.7 us (49%)
  starting transfers between devices  21.1 us (22%)
  waiting for transfers between devices  19.8 us (21%)
  local copies, waits for them, and re-layouts  4.84 us (5%)
  between operations  1.03 us (1%)
    pallas_call x1, Pallas kernels, per_device(): pl.pallas_call(functools.partial(embed_kernel, mem, nodes, per_owner), gr...  29.7 us
    all_to_all x1, waiting for transfers between devices, per_device(): lax.all_to_all(sums, everyone, split_axis=0, concat_axis=0, tiled=True)  7.9 us
    all_to_all x1, starting transfers between devices, per_device(): lax.all_to_all(asked, 'node', split_axis=0, concat_axis=0, tiled=True)  7.31 us
    all_to_all x1, starting transfers between devices, per_device(): lax.all_to_all(sums, everyone, split_axis=0, concat_axis=0, tiled=True)  6.58 us
    pallas_call x1, Pallas kernels, per_device(): pl.pallas_call(functools.partial(message_kernel, mem, per_owner, full, fe...  5.26 us
    all_to_all x1, waiting for transfers between devices, per_device(): lax.all_to_all(asked, 'node', split_axis=0, concat_axis=0, tiled=True)  4.3 us
    pallas_call x1, Pallas kernels, per_device(): pl.pallas_call(functools.partial(update_kernel, full, rest, feat), in_spe...  3.81 us
    ppermute x3, waiting for transfers between devices, per_device(): lax.ppermute(packed[k], 'feat', turn(k))  3.8 us
  transfers between devices with their start and end apart: 9, of which 5 were waited for; matrix products, arithmetic and copies ran while one was open for 4% of the time, Pallas kernels for 38%

profile of v2, /device:TPU:0, one launch (start us, length us, event | category | flops | bytes accessed | tf_op | source)
XLA Modules:
  0.0 93.2 jit_solution(15160280925256320755)
XLA Ops:
  0.6 0.7 reduce
  1.3 0.7 reshape.44
  2.0 7.3 %all-to-all-start = ((s32[8,1,192]{2,1,0:T(1,128)}), s32[8,1,192]{2,1,0:T(1,128)S(1)}, u32[]{:S(2)}, u32[]{:S(2)}) async-start(s32[8,1,192]{2,1,0:T(1,128)} %reshape.44), calls=%async_computation | async-start | bytes 16384 | tf_op jit(solution)/shard_map/all_to_all | solution.py:418
  9.3 0.7 copy-done.1
  10.0 1.5 %pack.1 = (bf16[176,1024]{1,0:T(8,128)(2,1)S(1)}, bf16[976,128]{1,0:T(8,128)(2,1)S(1)}, bf16[976,128]{1,0:T(8,128)(2,1)S(1)}, bf16[976,128]{1,0:T(8,128)(2,1)S(1)}, bf16[976,128]{1,0:T(8,128)(2,1)S(1)}) custom-call(s32[1]{0:T(128)} %bitcast.feat_ref, bf16[64,2048]{1,0:T(8,128)(2,1)} %bitcast.40, f32[3,43,700]{2,1,0:T(8,128)} %bitcast.38, ...), custom_call_target="tpu_custom_call" | custom-call | flops 100000000 | bytes 1000000 | tf_op jit(solution)/shard_map/pack/pallas_call | solution.py:433
  11.6 4.3 %all-to-all-done = s32[8,1,192]{2,1,0:T(1,128)S(1)} async-done(((s32[8,1,192]{2,1,0:T(1,128)}), s32[8,1,192]{2,1,0:T(1,128)S(1)}, u32[]{:S(2)}, u32[]{:S(2)}) %all-to-all-start) | async-done | bytes 6176 | tf_op jit(solution)/shard_map/all_to_all | solution.py:418
  15.9 1.6 %rows.1 = bf16[8,264,128]{2,1,0:T(8,128)(2,1)} custom-call(s32[8,192]{1,0:T(8,128)S(1)} %bitcast.27, bf16[176,1024]{1,0:T(8,128)(2,1)S(1)} %get-tuple-element.27.table_ref), custom_call_target="tpu_custom_call" | custom-call | flops 1000000000 | bytes 2000000 | tf_op jit(solution)/shard_map/rows/pallas_call | solution.py:450
  17.5 3.5 %all-to-all-start.1 = ((bf16[8,264,128]{2,1,0:T(8,128)(2,1)}), bf16[8,264,128]{2,1,0:T(8,128)(2,1)S(1)}, u32[]{:S(2)}, u32[]{:S(2)}) async-start(bf16[8,264,128]{2,1,0:T(8,128)(2,1)} %rows.1), calls=%async_computation.1 | async-start | bytes 1081344 | tf_op jit(solution)/shard_map/all_to_all | solution.py:459
  21.0 0.0 copy-done.9
  21.1 0.1 copy.30
  21.2 0.0 collective-permute-start.2
  21.2 0.0 copy-start.7
  21.2 0.0 copy-start.8
  21.2 0.0 copy-start
  21.2 0.0 copy-start.2
  21.2 3.8 %state.1.state_hbm = f32[4,43,1024]{2,1,0:T(8,128)} custom-call(f32[172,1024]{1,0:T(8,128)} %bitcast.37, f32[3,43,700]{2,1,0:T(8,128)} %bitcast.39, f32[3,43,172]{2,1,0:T(8,128)} %bitcast.49, f32[43,4]{1,0:T(8,128)S(1)} %bitcast.31), custom_call_target="tpu_custom_call" | custom-call | flops 3000000000 | bytes 3000000 | tf_op jit(solution)/shard_map/state/pallas_call | solution.py:461
  25.0 1.5 %collective-permute-start.1 = (s32[8,192]{1,0:T(8,128)S(1)}, s32[8,192]{1,0:T(8,128)S(1)}, u32[]{:S(2)}, u32[]{:S(2)}) collective-permute-start(s32[8,192]{1,0:T(8,128)S(1)} %bitcast.29), channel_id=1, source_target_pairs={{0,2},{1,3},{2,0},{3,1},{4,6},{5,7},{6,4},{7,5},{8,10},{9,11},{10,... | collective-permute-start | bytes 18440 | tf_op jit(solution)/shard_map/ppermute | solution.py:476
  26.5 0.2 collective-permute-start
  26.7 0.4 collective-permute-start.3
  27.1 1.5 %collective-permute-start.4 = (bf16[976,128]{1,0:T(8,128)(2,1)S(1)}, bf16[976,128]{1,0:T(8,128)(2,1)S(1)}, u32[]{:S(2)}, u32[]{:S(2)}) collective-permute-start(bf16[976,128]{1,0:T(8,128)(2,1)S(1)} %get-tuple-element.31), channel_id=1, source_target_pairs={{0,2},{1,3},{2,0},{3,1},{4,6},{5,7},{6,4},{7,5},{8,10},{9,11},{10,... | collective-permute-start | bytes 749576 | tf_op jit(solution)/shard_map/ppermute | solution.py:444
  28.7 0.0 collective-permute-done.2
  28.7 0.1 collective-permute-start.5
  28.7 1.6 %dynamic-slice_bitcast_fusion.own_hbm = f32[43,1024]{1,0:T(8,128)} fusion(f32[1024,172]{0,1:T(8,128)} %param.19, s32[]{:T(128)S(6)} %select_n.3), kind=kLoop, calls=%fused_computation | loop fusion | bytes 352260 | tf_op jit(solution)/shard_map/dynamic_slice | solution.py:475
  30.3 0.0 copy-done.7
  30.3 0.1 pad.7.freq_ref
  30.4 0.1 pad.8.phase_ref
  30.5 0.1 copy.33.freq_ref
  30.6 0.1 copy.34.phase_ref
  30.7 0.0 collective-permute-done.1
  30.7 0.0 collective-permute-done
  30.8 0.1 reshape.50
  30.9 3.7 %all-to-all-done.1.rows_ref = bf16[8,264,128]{2,1,0:T(8,128)(2,1)S(1)} async-done(((bf16[8,264,128]{2,1,0:T(8,128)(2,1)}), bf16[8,264,128]{2,1,0:T(8,128)(2,1)S(1)}, u32[]{:S(2)}, u32[]{:S(2)}) %all-to-all-start.1) | async-done | bytes 540704 | tf_op jit(solution)/shard_map/all_to_all | solution.py:459
  34.7 0.0 collective-permute-done.3.rest_refs_1_
  34.7 1.4 %collective-permute-done.4.rest_refs_2_ = bf16[976,128]{1,0:T(8,128)(2,1)S(1)} collective-permute-done((bf16[976,128]{1,0:T(8,128)(2,1)S(1)}, bf16[976,128]{1,0:T(8,128)(2,1)S(1)}, u32[]{:S(2)}, u32[]{:S(2)}) %collective-permute-start.4) | collective-permute-done | bytes 249888 | tf_op jit(solution)/shard_map/ppermute | solution.py:444
  36.1 2.4 %collective-permute-done.5.rest_refs_3_ = bf16[976,128]{1,0:T(8,128)(2,1)S(1)} collective-permute-done((bf16[976,128]{1,0:T(8,128)(2,1)S(1)}, bf16[976,128]{1,0:T(8,128)(2,1)S(1)}, u32[]{:S(2)}, u32[]{:S(2)}) %collective-permute-start.5) | collective-permute-done | bytes 249888 | tf_op jit(solution)/shard_map/ppermute | solution.py:444
  38.5 5.3 %messages.1 = (bf16[256,1536]{1,0:T(8,128)(2,1)}, bf16[32,200,128]{2,1,0:T(8,128)(2,1)}) custom-call(s32[1]{0:T(128)} %bitcast.feat_ref, bf16[8,264,128]{2,1,0:T(8,128)(2,1)S(1)} %all-to-all-done.1.rows_ref, s32[12,512]{1,0:T(8,128)S(1)} %bitcast.26, s32[1,512]{1,0:T(1,128)S(1)} %bitcast.33, f32[100,1]{1,0:T(8,128)S(1)} %copy.33.freq_ref, ...), custom_call_target="tpu_custom_call" | custom-call | flops 4000000000 | bytes 4000000 | tf_op jit(solution)/shard_map/messages/pallas_call | solution.py:487
  43.7 0.0 copy-start.6
  43.7 0.0 copy-start.5
  43.8 0.0 copy-start.3
  43.8 0.0 copy-start.4
  43.8 6.6 %all-to-all-start.2 = ((bf16[32,200,128]{2,1,0:T(8,128)(2,1)}), bf16[32,200,128]{2,1,0:T(8,128)(2,1)S(1)}, u32[]{:S(2)}, u32[]{:S(2)}) async-start(bf16[32,200,128]{2,1,0:T(8,128)(2,1)} %get-tuple-element.36), calls=%async_computation.2 | async-start | bytes 3276800 | tf_op jit(solution)/shard_map/all_to_all | solution.py:513
  50.4 0.1 copy.35.ref_ref
  50.5 0.1 copy.36.gap_ref
  50.7 0.1 copy.37.wm_ref
  50.8 29.7 %embed.1 = bf16[512,172]{1,0:T(8,128)(2,1)S(1)} custom-call(bf16[256,1536]{1,0:T(8,128)(2,1)} %get-tuple-element.33.table_ref, s32[512,12]{1,0:T(8,128)S(1)} %copy.35.ref_ref, s32[512,10]{1,0:T(8,128)S(1)} %copy.36.gap_ref, f32[1,256]{1,0:T(1,128)S(1)} %pad.7.freq_ref, f32[1,256]{1,0:T(1,128)S(1)} %pad.8.phase_ref, bf16[272,272]{1,0:T(8,128)(2,1)} %wq_ref.1, ...), custom_call_target="tpu_custom_call" | custom-call | flops 20000000000 | bytes 4000000 | tf_op jit(solution)/shard_map/embed/pallas_call | solution.py:517
  80.6 0.8 copy.38
  81.4 7.9 %all-to-all-done.2.recv_ref = bf16[32,200,128]{2,1,0:T(8,128)(2,1)S(1)} async-done(((bf16[32,200,128]{2,1,0:T(8,128)(2,1)}), bf16[32,200,128]{2,1,0:T(8,128)(2,1)S(1)}, u32[]{:S(2)}, u32[]{:S(2)}) %all-to-all-start.2) | async-done | bytes 1638432 | tf_op jit(solution)/shard_map/all_to_all | solution.py:513
  89.3 3.8 %update.1 = f32[43,1024]{1,0:T(8,128)} custom-call(s32[1]{0:T(128)} %bitcast.feat_ref, bf16[32,200,128]{2,1,0:T(8,128)(2,1)S(1)} %all-to-all-done.2.recv_ref, s32[8,1,768]{2,1,0:T(1,128)S(1)} %pad_add_fusion.1.ids_ref, f32[4,43,1024]{2,1,0:T(8,128)} %state.1.state_hbm, f32[43,1024]{1,0:T(8,128)} %dynamic-slice_bitcast_fusion.own_hbm), custom_call_target="tpu_custom_call" | custom-call | flops 4000000000 | bytes 4000000 | tf_op jit(solution)/shard_map/update/pallas_call | solution.py:559
  (16 shorter events, 0.1 us)
Async XLA Ops:
  2.0 13.8 %all-to-all-start = ((s32[8,1,192]{2,1,0:T(1,128)}), s32[8,1,192]{2,1,0:T(1,128)S(1)}, u32[]{:S(2)}, u32[]{:S(2)}) async-start(s32[8,1,192]{2,1,0:T(1,128)} %reshape.44), calls=%async_computation | async-start | bytes 16384 | tf_op jit(solution)/shard_map/all_to_all | solution.py:418
  9.3 0.7 copy-start.1
  15.9 5.2 %copy-start.9 = (f32[4,43]{1,0:T(4,128)S(1)}, f32[4,43]{1,0:T(4,128)}, u32[]{:S(2)}) copy-start(f32[4,43]{1,0:T(4,128)} %param.37) | copy-start | bytes 2068
  17.5 17.1 %all-to-all-start.1 = ((bf16[8,264,128]{2,1,0:T(8,128)(2,1)}), bf16[8,264,128]{2,1,0:T(8,128)(2,1)S(1)}, u32[]{:S(2)}, u32[]{:S(2)}) async-start(bf16[8,264,128]{2,1,0:T(8,128)(2,1)} %rows.1), calls=%async_computation.1 | async-start | bytes 1081344 | tf_op jit(solution)/shard_map/all_to_all | solution.py:459
  21.2 7.5 %collective-permute-start.2 = (s32[8,192]{1,0:T(8,128)S(1)}, s32[8,192]{1,0:T(8,128)S(1)}, u32[]{:S(2)}, u32[]{:S(2)}) collective-permute-start(s32[8,192]{1,0:T(8,128)S(1)} %bitcast.28), channel_id=1, source_target_pairs={{0,3},{1,0},{2,1},{3,2},{4,7},{5,4},{6,5},{7,6},{8,11},{9,8},{10,9... | collective-permute-start | bytes 18440 | tf_op jit(solution)/shard_map/ppermute | solution.py:476
  21.2 9.2 %copy-start.7 = (f32[100]{0:T(128)S(1)}, f32[100]{0:T(128)}, u32[]{:S(2)}) copy-start(f32[100]{0:T(128)} %param.26) | copy-start | bytes 1204
  21.2 9.2 %copy-start.8 = (f32[100]{0:T(128)S(1)}, f32[100]{0:T(128)}, u32[]{:S(2)}) copy-start(f32[100]{0:T(128)} %param.27) | copy-start | bytes 1204
  21.2 17.3 %copy-start = (s32[512,12]{0,1:T(8,128)S(1)}, s32[512,12]{0,1:T(8,128)}, u32[]{:S(2)}) copy-start(s32[512,12]{0,1:T(8,128)} %param.24) | copy-start | bytes 73732
  21.2 17.3 %copy-start.2 = (s32[512]{0:T(512)S(1)}, s32[512]{0:T(512)}, u32[]{:S(2)}) copy-start(s32[512]{0:T(512)} %param.21) | copy-start | bytes 6148
  25.0 5.7 %collective-permute-start.1 = (s32[8,192]{1,0:T(8,128)S(1)}, s32[8,192]{1,0:T(8,128)S(1)}, u32[]{:S(2)}, u32[]{:S(2)}) collective-permute-start(s32[8,192]{1,0:T(8,128)S(1)} %bitcast.29), channel_id=1, source_target_pairs={{0,2},{1,3},{2,0},{3,1},{4,6},{5,7},{6,4},{7,5},{8,10},{9,11},{10,... | collective-permute-start | bytes 18440 | tf_op jit(solution)/shard_map/ppermute | solution.py:476
  26.5 4.2 %collective-permute-start = (s32[8,192]{1,0:T(8,128)S(1)}, s32[8,192]{1,0:T(8,128)S(1)}, u32[]{:S(2)}, u32[]{:S(2)}) collective-permute-start(s32[8,192]{1,0:T(8,128)S(1)} %bitcast.30), channel_id=1, source_target_pairs={{0,1},{1,2},{2,3},{3,0},{4,5},{5,6},{6,7},{7,4},{8,9},{9,10},{10,1... | collective-permute-start | bytes 18440 | tf_op jit(solution)/shard_map/ppermute | solution.py:476
  26.7 7.9 %collective-permute-start.3 = (bf16[976,128]{1,0:T(8,128)(2,1)S(1)}, bf16[976,128]{1,0:T(8,128)(2,1)S(1)}, u32[]{:S(2)}, u32[]{:S(2)}) collective-permute-start(bf16[976,128]{1,0:T(8,128)(2,1)S(1)} %get-tuple-element.30), channel_id=1, source_target_pairs={{0,1},{1,2},{2,3},{3,0},{4,5},{5,6},{6,7},{7,4},{8,9},{9,10},{10,1... | collective-permute-start | bytes 749576 | tf_op jit(solution)/shard_map/ppermute | solution.py:444
  27.1 8.9 %collective-permute-start.4 = (bf16[976,128]{1,0:T(8,128)(2,1)S(1)}, bf16[976,128]{1,0:T(8,128)(2,1)S(1)}, u32[]{:S(2)}, u32[]{:S(2)}) collective-permute-start(bf16[976,128]{1,0:T(8,128)(2,1)S(1)} %get-tuple-element.31), channel_id=1, source_target_pairs={{0,2},{1,3},{2,0},{3,1},{4,6},{5,7},{6,4},{7,5},{8,10},{9,11},{10,... | collective-permute-start | bytes 749576 | tf_op jit(solution)/shard_map/ppermute | solution.py:444
  28.7 9.8 %collective-permute-start.5 = (bf16[976,128]{1,0:T(8,128)(2,1)S(1)}, bf16[976,128]{1,0:T(8,128)(2,1)S(1)}, u32[]{:S(2)}, u32[]{:S(2)}) collective-permute-start(bf16[976,128]{1,0:T(8,128)(2,1)S(1)} %get-tuple-element.32), channel_id=1, source_target_pairs={{0,3},{1,0},{2,1},{3,2},{4,7},{5,4},{6,5},{7,6},{8,11},{9,8},{10,9... | collective-permute-start | bytes 749576 | tf_op jit(solution)/shard_map/ppermute | solution.py:444
  43.7 6.8 %copy-start.6 = (s32[512,10]{0,1:T(8,128)S(1)}, s32[512,10]{0,1:T(8,128)}, u32[]{:S(2)}) copy-start(s32[512,10]{0,1:T(8,128)} %param.22) | copy-start | bytes 61444
  43.7 6.9 %copy-start.5 = (bf16[444,172]{0,1:T(8,128)(2,1)S(1)}, bf16[444,172]{0,1:T(8,128)(2,1)}, u32[]{:S(2)}) copy-start(bf16[444,172]{0,1:T(8,128)(2,1)} %param.31) | copy-start | bytes 458212
  43.8 7.1 %copy-start.3 = (f32[172]{0:T(256)S(1)}, f32[172]{0:T(256)}, u32[]{:S(2)}) copy-start(f32[172]{0:T(256)} %param.32) | copy-start | bytes 2068
  43.8 7.1 %copy-start.4 = (f32[172]{0:T(256)S(1)}, f32[172]{0:T(256)}, u32[]{:S(2)}) copy-start(f32[172]{0:T(256)} %param.34) | copy-start | bytes 2068
  43.8 45.5 %all-to-all-start.2 = ((bf16[32,200,128]{2,1,0:T(8,128)(2,1)}), bf16[32,200,128]{2,1,0:T(8,128)(2,1)S(1)}, u32[]{:S(2)}, u32[]{:S(2)}) async-start(bf16[32,200,128]{2,1,0:T(8,128)(2,1)} %get-tuple-element.36), calls=%async_computation.2 | async-start | bytes 3276800 | tf_op jit(solution)/shard_map/all_to_all | solution.py:513

commit v3 on v2

--- a/solution.py
+++ b/solution.py
@@ -195,22 +195,23 @@
         for c in range(events // LANES):
             edge_ref[pl.ds(at, own), c * LANES : (c + 1) * LANES] = pack_refs[k][c * own : (c + 1) * own, :]
     table = table_ref[0:height, :]
-    slot_of = iota((slots, events), 0)
     place = places_of(slot_ref[0:2, :], nodes, per_owner)
-    hots = [hot(slot_of == place[i : i + 1, :]) for i in range(2)]
-    found = [mm(table, h) for h in hots]
+    place = jnp.concatenate([place[0:1, :], place[1:2, :]], 1)
+    hots = hot(iota((slots, 2 * events), 0) == place)
+    both = mm(table, hots)
+    found = [both[:, i * events : (i + 1) * events] for i in range(2)]
     freq = freq_ref[...]
     phase = phase_ref[...]
     by_edge = mm(w_ref[:, EDGE_AT:COLS], edge_ref[...])
     height_all = w_ref.shape[0]
     ones = iota((height_all, events), 0) == feat * LANES + feat
-    sums = None
+    sent = []
     for i in range(2):
         stamps = found[i][mem : mem + 1, :] * float(1 << STAMP_SHIFT) + found[i][mem + 1 : mem + 2, :]
         code = cosine(freq * (time_ref[...].astype(f32) - stamps) + phase).astype(bf16)
-        sent = mm(w_ref[:, 0:height], found[1 - i].astype(bf16)) + mm(w_ref[:, TIME_AT : TIME_AT + time], code) + by_edge
-        part = mm_nt(jnp.where(ones, 1.0, sent).astype(bf16), hots[i])
-        sums = part if sums is None else sums + part
+        part = mm(w_ref[:, 0:height], found[1 - i].astype(bf16)) + mm(w_ref[:, TIME_AT : TIME_AT + time], code) + by_edge
+        sent.append(jnp.where(ones, 1.0, part).astype(bf16))
+    sums = mm_nt(jnp.concatenate(sent, 1), hots)
     extra = sums[feat * LANES :, :]
     hits = extra[feat : feat + 1, :]
     high = jnp.floor(hits * (1.0 / HIT_BASE))
@@ -439,7 +440,7 @@
         compiler_params=modest(),
         name="pack",
     )(here_line, off_chip(edge_feat.T), off_chip(w_input_t), off_chip(memory_t), last_update.reshape(1, rows))
-    asked, table, *packed = lax.optimization_barrier((asked, table, *packed))
+    asked, table = lax.optimization_barrier((asked, table))
     turn = lambda k: [(i, (i + k) % feat) for i in range(feat)]
     packed = [packed[0]] + [lax.ppermute(packed[k], "feat", turn(k)) for k in range(1, feat)]
 
@@ -471,7 +472,8 @@
     phase_line = phase_shift.reshape(1, time)
     shift = mem - LANES
     spread = ((0, 0), (shift, 2 * LANES - shift - time))
-    freq_wide, phase_wide = jnp.pad(freq_line, spread), jnp.pad(phase_line, spread)
+    freq_wide = jnp.pad(freq_line, spread)
+    phase_wide = jnp.pad(phase_line, spread)
     own_cols = lax.dynamic_slice_in_dim(memory_t, here * width, width, 0)
     asked = jnp.stack([asked] + [lax.ppermute(asked, "feat", turn(k)) for k in range(1, feat)], 1)
     ids = [asked[:, :, c * LANES : (c + 1) * LANES].reshape(nodes, 1, feat * LANES) for c in range(full)]

time: 93.8 us -> 91.8 us (0.979)
  waiting for transfers between devices: 19.8 us -> 17.8 us
    ppermute x3, waiting for transfers between devices: 0.01 us -> 5.64 us  [per_device(): lax.ppermute(asked, 'feat', turn(k))]
    ppermute x3, waiting for transfers between devices: 3.8 us -> 0.01 us  [per_device(): lax.ppermute(packed[k], 'feat', turn(k))]
    all_to_all x1, waiting for transfers between devices: 3.75 us -> 0.01 us  [per_device(): lax.all_to_all(found, 'node', split_axis=0, concat_axis=0, tiled=True)]
    ppermute x3, starting transfers between devices: 1.98 us -> 3 us  [per_device(): lax.ppermute(packed[k], 'feat', turn(k))]
  transfers between devices with their start and end apart: 9 -> 9, of which waited for: 5 -> 4; matrix products, arithmetic and copies ran while one was open for 4% -> 4% of each run, Pallas kernels for 38% -> 38%
where the time goes in v3:
time: 91.8 us; the launch traced here: 91.3 us
  Pallas kernels  45.7 us (50%)
  starting transfers between devices  21.1 us (23%)
  waiting for transfers between devices  17.8 us (19%)
  local copies, waits for them, and re-layouts  4.84 us (5%)
  between operations  1.06 us (1%)
    pallas_call x1, Pallas kernels, per_device(): pl.pallas_call(functools.partial(embed_kernel, mem, nodes, per_owner), gr...  29.7 us
    all_to_all x1, waiting for transfers between devices, per_device(): lax.all_to_all(sums, everyone, split_axis=0, concat_axis=0, tiled=True)  7.89 us
    all_to_all x1, starting transfers between devices, per_device(): lax.all_to_all(asked, 'node', split_axis=0, concat_axis=0, tiled=True)  7.31 us
    all_to_all x1, starting transfers between devices, per_device(): lax.all_to_all(sums, everyone, split_axis=0, concat_axis=0, tiled=True)  5.7 us
    ppermute x3, waiting for transfers between devices, per_device(): lax.ppermute(asked, 'feat', turn(k))  5.64 us
    pallas_call x1, Pallas kernels, per_device(): pl.pallas_call(functools.partial(message_kernel, mem, per_owner, full, fe...  5.23 us
    all_to_all x1, waiting for transfers between devices, per_device(): lax.all_to_all(asked, 'node', split_axis=0, concat_axis=0, tiled=True)  4.3 us
    pallas_call x1, Pallas kernels, per_device(): pl.pallas_call(functools.partial(update_kernel, full, rest, feat), in_spe...  3.81 us
  transfers between devices with their start and end apart: 9, of which 4 were waited for; matrix products, arithmetic and copies ran while one was open for 4% of the time, Pallas kernels for 38%

profile of v3, /device:TPU:0, one launch (start us, length us, event | category | flops | bytes accessed | tf_op | source)
XLA Modules:
  0.0 91.3 jit_solution(9882383319465155932)
XLA Ops:
  0.6 0.7 reduce
  1.3 0.7 reshape.44
  2.0 7.3 %all-to-all-start = ((s32[8,1,192]{2,1,0:T(1,128)}), s32[8,1,192]{2,1,0:T(1,128)S(1)}, u32[]{:S(2)}, u32[]{:S(2)}) async-start(s32[8,1,192]{2,1,0:T(1,128)} %reshape.44), calls=%async_computation | async-start | bytes 16384 | tf_op jit(solution)/shard_map/all_to_all | solution.py:419
  9.3 0.7 copy-done.1
  10.0 1.5 %pack.1 = (bf16[176,1024]{1,0:T(8,128)(2,1)S(1)}, bf16[976,128]{1,0:T(8,128)(2,1)S(1)}, bf16[976,128]{1,0:T(8,128)(2,1)S(1)}, bf16[976,128]{1,0:T(8,128)(2,1)S(1)}, bf16[976,128]{1,0:T(8,128)(2,1)S(1)}) custom-call(s32[1]{0:T(128)} %bitcast.feat_ref, bf16[64,2048]{1,0:T(8,128)(2,1)} %bitcast.40, f32[3,43,700]{2,1,0:T(8,128)} %bitcast.38, ...), custom_call_target="tpu_custom_call" | custom-call | flops 100000000 | bytes 1000000 | tf_op jit(solution)/shard_map/pack/pallas_call | solution.py:434
  11.6 4.3 %all-to-all-done = s32[8,1,192]{2,1,0:T(1,128)S(1)} async-done(((s32[8,1,192]{2,1,0:T(1,128)}), s32[8,1,192]{2,1,0:T(1,128)S(1)}, u32[]{:S(2)}, u32[]{:S(2)}) %all-to-all-start) | async-done | bytes 6176 | tf_op jit(solution)/shard_map/all_to_all | solution.py:419
  15.9 1.6 %rows.1 = bf16[8,264,128]{2,1,0:T(8,128)(2,1)} custom-call(s32[8,192]{1,0:T(8,128)S(1)} %bitcast.27, bf16[176,1024]{1,0:T(8,128)(2,1)S(1)} %get-tuple-element.19.table_ref), custom_call_target="tpu_custom_call" | custom-call | flops 1000000000 | bytes 2000000 | tf_op jit(solution)/shard_map/rows/pallas_call | solution.py:451
  17.5 3.5 %all-to-all-start.1 = ((bf16[8,264,128]{2,1,0:T(8,128)(2,1)}), bf16[8,264,128]{2,1,0:T(8,128)(2,1)S(1)}, u32[]{:S(2)}, u32[]{:S(2)}) async-start(bf16[8,264,128]{2,1,0:T(8,128)(2,1)} %rows.1), calls=%async_computation.1 | async-start | bytes 1081344 | tf_op jit(solution)/shard_map/all_to_all | solution.py:460
  21.0 0.1 collective-permute-start.3
  21.1 1.6 %collective-permute-start.4 = (bf16[976,128]{1,0:T(8,128)(2,1)S(1)}, bf16[976,128]{1,0:T(8,128)(2,1)S(1)}, u32[]{:S(2)}, u32[]{:S(2)}) collective-permute-start(bf16[976,128]{1,0:T(8,128)(2,1)S(1)} %get-tuple-element.23), channel_id=1, source_target_pairs={{0,2},{1,3},{2,0},{3,1},{4,6},{5,7},{6,4},{7,5},{8,10},{9,11},{10,... | collective-permute-start | bytes 749576 | tf_op jit(solution)/shard_map/ppermute | solution.py:445
  22.7 1.4 %collective-permute-start.5 = (bf16[976,128]{1,0:T(8,128)(2,1)S(1)}, bf16[976,128]{1,0:T(8,128)(2,1)S(1)}, u32[]{:S(2)}, u32[]{:S(2)}) collective-permute-start(bf16[976,128]{1,0:T(8,128)(2,1)S(1)} %get-tuple-element.24), channel_id=1, source_target_pairs={{0,3},{1,0},{2,1},{3,2},{4,7},{5,4},{6,5},{7,6},{8,11},{9,8},{10,9... | collective-permute-start | bytes 749576 | tf_op jit(solution)/shard_map/ppermute | solution.py:445
  24.1 0.0 copy-done.9
  24.1 0.1 copy.30
  24.2 0.0 collective-permute-start.2
  24.2 0.0 copy-start.7
  24.2 0.0 copy-start.8
  24.2 0.0 copy-start
  24.2 0.0 copy-start.2
  24.2 3.8 %state.1.state_hbm = f32[4,43,1024]{2,1,0:T(8,128)} custom-call(f32[172,1024]{1,0:T(8,128)} %bitcast.37, f32[3,43,700]{2,1,0:T(8,128)} %bitcast.39, f32[3,43,172]{2,1,0:T(8,128)} %bitcast.49, f32[43,4]{1,0:T(8,128)S(1)} %bitcast.31), custom_call_target="tpu_custom_call" | custom-call | flops 3000000000 | bytes 3000000 | tf_op jit(solution)/shard_map/state/pallas_call | solution.py:462
  28.0 0.7 collective-permute-start.1
  28.8 5.2 %collective-permute-done.2 = s32[8,192]{1,0:T(8,128)S(1)} collective-permute-done((s32[8,192]{1,0:T(8,128)S(1)}, s32[8,192]{1,0:T(8,128)S(1)}, u32[]{:S(2)}, u32[]{:S(2)}) %collective-permute-start.2) | collective-permute-done | bytes 6176 | tf_op jit(solution)/shard_map/ppermute | solution.py:478
  34.0 0.8 collective-permute-start
  34.8 1.6 %dynamic-slice_bitcast_fusion.own_hbm = f32[43,1024]{1,0:T(8,128)} fusion(f32[1024,172]{0,1:T(8,128)} %param.19, s32[]{:T(128)S(6)} %select_n.3), kind=kLoop, calls=%fused_computation | loop fusion | bytes 352260 | tf_op jit(solution)/shard_map/dynamic_slice | solution.py:477
  36.4 0.0 copy-done.7
  36.4 0.1 pad.7.freq_ref
  36.5 0.1 pad.8.phase_ref
  36.6 0.1 copy.33.freq_ref
  36.7 0.1 copy.34.phase_ref
  36.8 0.0 collective-permute-done.1
  36.8 0.4 collective-permute-done
  37.3 0.1 reshape.50
  37.4 0.0 all-to-all-done.1.rows_ref
  37.4 0.0 collective-permute-done.3.rest_refs_1_
  37.4 0.0 collective-permute-done.4.rest_refs_2_
  37.4 0.0 collective-permute-done.5.rest_refs_3_
  37.4 5.2 %messages.1 = (bf16[256,1536]{1,0:T(8,128)(2,1)}, bf16[32,200,128]{2,1,0:T(8,128)(2,1)}) custom-call(s32[1]{0:T(128)} %bitcast.feat_ref, bf16[8,264,128]{2,1,0:T(8,128)(2,1)S(1)} %all-to-all-done.1.rows_ref, s32[12,512]{1,0:T(8,128)S(1)} %bitcast.26, s32[1,512]{1,0:T(1,128)S(1)} %bitcast.33, f32[100,1]{1,0:T(8,128)S(1)} %copy.33.freq_ref, ...), custom_call_target="tpu_custom_call" | custom-call | flops 4000000000 | bytes 4000000 | tf_op jit(solution)/shard_map/messages/pallas_call | solution.py:489
  42.7 0.0 copy-start.6
  42.7 0.0 copy-start.5
  42.7 0.0 copy-start.3
  42.7 0.0 copy-start.4
  42.7 5.7 %all-to-all-start.2 = ((bf16[32,200,128]{2,1,0:T(8,128)(2,1)}), bf16[32,200,128]{2,1,0:T(8,128)(2,1)S(1)}, u32[]{:S(2)}, u32[]{:S(2)}) async-start(bf16[32,200,128]{2,1,0:T(8,128)(2,1)} %get-tuple-element.28), calls=%async_computation.2 | async-start | bytes 3276800 | tf_op jit(solution)/shard_map/all_to_all | solution.py:515
  48.4 0.1 copy.35.ref_ref
  48.6 0.1 copy.36.gap_ref
  48.7 0.1 copy.37.wm_ref
  48.9 29.7 %embed.1 = bf16[512,172]{1,0:T(8,128)(2,1)S(1)} custom-call(bf16[256,1536]{1,0:T(8,128)(2,1)} %get-tuple-element.25.table_ref, s32[512,12]{1,0:T(8,128)S(1)} %copy.35.ref_ref, s32[512,10]{1,0:T(8,128)S(1)} %copy.36.gap_ref, f32[1,256]{1,0:T(1,128)S(1)} %pad.7.freq_ref, f32[1,256]{1,0:T(1,128)S(1)} %pad.8.phase_ref, bf16[272,272]{1,0:T(8,128)(2,1)} %wq_ref.1, ...), custom_call_target="tpu_custom_call" | custom-call | flops 20000000000 | bytes 4000000 | tf_op jit(solution)/shard_map/embed/pallas_call | solution.py:519
  78.6 0.8 copy.38
  79.4 7.9 %all-to-all-done.2.recv_ref = bf16[32,200,128]{2,1,0:T(8,128)(2,1)S(1)} async-done(((bf16[32,200,128]{2,1,0:T(8,128)(2,1)}), bf16[32,200,128]{2,1,0:T(8,128)(2,1)S(1)}, u32[]{:S(2)}, u32[]{:S(2)}) %all-to-all-start.2) | async-done | bytes 1638432 | tf_op jit(solution)/shard_map/all_to_all | solution.py:515
  87.3 3.8 %update.1 = f32[43,1024]{1,0:T(8,128)} custom-call(s32[1]{0:T(128)} %bitcast.feat_ref, bf16[32,200,128]{2,1,0:T(8,128)(2,1)S(1)} %all-to-all-done.2.recv_ref, s32[8,1,768]{2,1,0:T(1,128)S(1)} %pad_add_fusion.1.ids_ref, f32[4,43,1024]{2,1,0:T(8,128)} %state.1.state_hbm, f32[43,1024]{1,0:T(8,128)} %dynamic-slice_bitcast_fusion.own_hbm), custom_call_target="tpu_custom_call" | custom-call | flops 4000000000 | bytes 4000000 | tf_op jit(solution)/shard_map/update/pallas_call | solution.py:561
  (16 shorter events, 0.1 us)
Async XLA Ops:
  2.0 13.8 %all-to-all-start = ((s32[8,1,192]{2,1,0:T(1,128)}), s32[8,1,192]{2,1,0:T(1,128)S(1)}, u32[]{:S(2)}, u32[]{:S(2)}) async-start(s32[8,1,192]{2,1,0:T(1,128)} %reshape.44), calls=%async_computation | async-start | bytes 16384 | tf_op jit(solution)/shard_map/all_to_all | solution.py:419
  9.3 0.7 copy-start.1
  15.9 8.2 %copy-start.9 = (f32[4,43]{1,0:T(4,128)S(1)}, f32[4,43]{1,0:T(4,128)}, u32[]{:S(2)}) copy-start(f32[4,43]{1,0:T(4,128)} %param.37) | copy-start | bytes 2068
  17.5 19.9 %all-to-all-start.1 = ((bf16[8,264,128]{2,1,0:T(8,128)(2,1)}), bf16[8,264,128]{2,1,0:T(8,128)(2,1)S(1)}, u32[]{:S(2)}, u32[]{:S(2)}) async-start(bf16[8,264,128]{2,1,0:T(8,128)(2,1)} %rows.1), calls=%async_computation.1 | async-start | bytes 1081344 | tf_op jit(solution)/shard_map/all_to_all | solution.py:460
  21.0 16.3 %collective-permute-start.3 = (bf16[976,128]{1,0:T(8,128)(2,1)S(1)}, bf16[976,128]{1,0:T(8,128)(2,1)S(1)}, u32[]{:S(2)}, u32[]{:S(2)}) collective-permute-start(bf16[976,128]{1,0:T(8,128)(2,1)S(1)} %get-tuple-element.22), channel_id=1, source_target_pairs={{0,1},{1,2},{2,3},{3,0},{4,5},{5,6},{6,7},{7,4},{8,9},{9,10},{10,1... | collective-permute-start | bytes 749576 | tf_op jit(solution)/shard_map/ppermute | solution.py:445
  21.1 16.3 %collective-permute-start.4 = (bf16[976,128]{1,0:T(8,128)(2,1)S(1)}, bf16[976,128]{1,0:T(8,128)(2,1)S(1)}, u32[]{:S(2)}, u32[]{:S(2)}) collective-permute-start(bf16[976,128]{1,0:T(8,128)(2,1)S(1)} %get-tuple-element.23), channel_id=1, source_target_pairs={{0,2},{1,3},{2,0},{3,1},{4,6},{5,7},{6,4},{7,5},{8,10},{9,11},{10,... | collective-permute-start | bytes 749576 | tf_op jit(solution)/shard_map/ppermute | solution.py:445
  22.7 14.7 %collective-permute-start.5 = (bf16[976,128]{1,0:T(8,128)(2,1)S(1)}, bf16[976,128]{1,0:T(8,128)(2,1)S(1)}, u32[]{:S(2)}, u32[]{:S(2)}) collective-permute-start(bf16[976,128]{1,0:T(8,128)(2,1)S(1)} %get-tuple-element.24), channel_id=1, source_target_pairs={{0,3},{1,0},{2,1},{3,2},{4,7},{5,4},{6,5},{7,6},{8,11},{9,8},{10,9... | collective-permute-start | bytes 749576 | tf_op jit(solution)/shard_map/ppermute | solution.py:445
  24.2 9.8 %collective-permute-start.2 = (s32[8,192]{1,0:T(8,128)S(1)}, s32[8,192]{1,0:T(8,128)S(1)}, u32[]{:S(2)}, u32[]{:S(2)}) collective-permute-start(s32[8,192]{1,0:T(8,128)S(1)} %bitcast.28), channel_id=1, source_target_pairs={{0,3},{1,0},{2,1},{3,2},{4,7},{5,4},{6,5},{7,6},{8,11},{9,8},{10,9... | collective-permute-start | bytes 18440 | tf_op jit(solution)/shard_map/ppermute | solution.py:478
  24.2 12.2 %copy-start.7 = (f32[100]{0:T(128)S(1)}, f32[100]{0:T(128)}, u32[]{:S(2)}) copy-start(f32[100]{0:T(128)} %param.26) | copy-start | bytes 1204
  24.2 12.3 %copy-start.8 = (f32[100]{0:T(128)S(1)}, f32[100]{0:T(128)}, u32[]{:S(2)}) copy-start(f32[100]{0:T(128)} %param.27) | copy-start | bytes 1204
  24.2 13.2 %copy-start = (s32[512,12]{0,1:T(8,128)S(1)}, s32[512,12]{0,1:T(8,128)}, u32[]{:S(2)}) copy-start(s32[512,12]{0,1:T(8,128)} %param.24) | copy-start | bytes 73732
  24.2 13.2 %copy-start.2 = (s32[512]{0:T(512)S(1)}, s32[512]{0:T(512)}, u32[]{:S(2)}) copy-start(s32[512]{0:T(512)} %param.21) | copy-start | bytes 6148
  28.0 8.8 %collective-permute-start.1 = (s32[8,192]{1,0:T(8,128)S(1)}, s32[8,192]{1,0:T(8,128)S(1)}, u32[]{:S(2)}, u32[]{:S(2)}) collective-permute-start(s32[8,192]{1,0:T(8,128)S(1)} %bitcast.29), channel_id=1, source_target_pairs={{0,2},{1,3},{2,0},{3,1},{4,6},{5,7},{6,4},{7,5},{8,10},{9,11},{10,... | collective-permute-start | bytes 18440 | tf_op jit(solution)/shard_map/ppermute | solution.py:478
  34.0 3.2 %collective-permute-start = (s32[8,192]{1,0:T(8,128)S(1)}, s32[8,192]{1,0:T(8,128)S(1)}, u32[]{:S(2)}, u32[]{:S(2)}) collective-permute-start(s32[8,192]{1,0:T(8,128)S(1)} %bitcast.30), channel_id=1, source_target_pairs={{0,1},{1,2},{2,3},{3,0},{4,5},{5,6},{6,7},{7,4},{8,9},{9,10},{10,1... | collective-permute-start | bytes 18440 | tf_op jit(solution)/shard_map/ppermute | solution.py:478
  42.7 5.9 %copy-start.6 = (s32[512,10]{0,1:T(8,128)S(1)}, s32[512,10]{0,1:T(8,128)}, u32[]{:S(2)}) copy-start(s32[512,10]{0,1:T(8,128)} %param.22) | copy-start | bytes 61444
  42.7 6.0 %copy-start.5 = (bf16[444,172]{0,1:T(8,128)(2,1)S(1)}, bf16[444,172]{0,1:T(8,128)(2,1)}, u32[]{:S(2)}) copy-start(bf16[444,172]{0,1:T(8,128)(2,1)} %param.31) | copy-start | bytes 458212
  42.7 6.2 %copy-start.3 = (f32[172]{0:T(256)S(1)}, f32[172]{0:T(256)}, u32[]{:S(2)}) copy-start(f32[172]{0:T(256)} %param.32) | copy-start | bytes 2068
  42.7 6.2 %copy-start.4 = (f32[172]{0:T(256)S(1)}, f32[172]{0:T(256)}, u32[]{:S(2)}) copy-start(f32[172]{0:T(256)} %param.34) | copy-start | bytes 2068
  42.7 44.6 %all-to-all-start.2 = ((bf16[32,200,128]{2,1,0:T(8,128)(2,1)}), bf16[32,200,128]{2,1,0:T(8,128)(2,1)S(1)}, u32[]{:S(2)}, u32[]{:S(2)}) async-start(bf16[32,200,128]{2,1,0:T(8,128)(2,1)} %get-tuple-element.28), calls=%async_computation.2 | async-start | bytes 3276800 | tf_op jit(solution)/shard_map/all_to_all | solution.py:515

commit v4 on v3

--- a/solution.py
+++ b/solution.py
@@ -338,10 +338,12 @@
                 ends = [tails[b + j][full * GROUP : (full + 1) * GROUP] for j in range(2)]
                 side.append(jnp.where(left(ends[0].shape), ends[0], swapped(ends[1])))
         side = jnp.concatenate(side, 1)
-        side = jnp.concatenate([side, jnp.zeros((16 - GROUP, side.shape[1]), f32)], 0).astype(bf16)
-        data = jnp.concatenate([jnp.concatenate(main, 1), side], 0)
+        side = jnp.concatenate([side, jnp.zeros((8 - GROUP, side.shape[1]), f32)], 0)
+        main = jnp.concatenate(main, 1)
         ids = ids_ref[i]
-        data = jnp.concatenate([data * hot((ids >= h * rows) & (ids < (h + 1) * rows)) for h in range(SPLIT)], 0)
+        masks = [jnp.where((ids >= h * rows) & (ids < (h + 1) * rows), 1.0, 0.0) for h in range(SPLIT)]
+        tails = jnp.concatenate([side * m for m in masks], 0).astype(bf16)
+        data = jnp.concatenate([main * m.astype(bf16) for m in masks] + [tails], 0)
         acc_ref[...] += mm_nt(data, hot(iota((rows, ids.shape[1]), 0) == ids % rows))
         return carry
 
@@ -349,8 +351,10 @@
     lax.fori_loop(0, steps, step, 0, unroll=steps <= 8)
     for load in loads:
         load.wait()
-    height = acc_ref.shape[0] // SPLIT
-    acc = jnp.concatenate([acc_ref[h * height : (h + 1) * height, :] for h in range(SPLIT)], 1)
+    ends = SPLIT * LANES
+    top = jnp.concatenate([acc_ref[h * LANES : (h + 1) * LANES, :] for h in range(SPLIT)], 1)
+    low = jnp.concatenate([acc_ref[ends + h * 8 : ends + (h + 1) * 8, :] for h in range(SPLIT)], 1)
+    acc = jnp.concatenate([top, low], 0)
     at = 3 * width
     hits = acc[at : at + 1, :] * HIT_BASE + acc[at + 1 : at + 2, :]
     scale = 1.0 / jnp.maximum(hits, 1.0)
@@ -564,7 +568,7 @@
         out_specs=vmem,
         out_shape=jax.ShapeDtypeStruct((width, rows), f32),
         scratch_shapes=[
-            pltpu.VMEM((SPLIT * (LANES + 16), rows // SPLIT), f32),
+            pltpu.VMEM((SPLIT * (LANES + 8), rows // SPLIT), f32),
             pltpu.VMEM((4, width, rows), f32),
             pltpu.VMEM((width, rows), f32),
             pltpu.SemaphoreType.DMA((2,)),

time: 91.8 us -> 91.7 us (level)
  no operation moved by 1% of the time
where the time goes in v4:
time: 91.7 us; the launch traced here: 91.2 us
  Pallas kernels  45.6 us (50%)
  starting transfers between devices  21.1 us (23%)
  waiting for transfers between devices  17.8 us (19%)
  local copies, waits for them, and re-layouts  4.84 us (5%)
  between operations  1.06 us (1%)
    pallas_call x1, Pallas kernels, per_device(): pl.pallas_call(functools.partial(embed_kernel, mem, nodes, per_owner), gr...  29.7 us
    all_to_all x1, waiting for transfers between devices, per_device(): lax.all_to_all(sums, everyone, split_axis=0, concat_axis=0, tiled=True)  7.89 us
    all_to_all x1, starting transfers between devices, per_device(): lax.all_to_all(asked, 'node', split_axis=0, concat_axis=0, tiled=True)  7.31 us
    all_to_all x1, starting transfers between devices, per_device(): lax.all_to_all(sums, everyone, split_axis=0, concat_axis=0, tiled=True)  5.7 us
    ppermute x3, waiting for transfers between devices, per_device(): lax.ppermute(asked, 'feat', turn(k))  5.64 us
    pallas_call x1, Pallas kernels, per_device(): pl.pallas_call(functools.partial(message_kernel, mem, per_owner, full, fe...  5.23 us
    all_to_all x1, waiting for transfers between devices, per_device(): lax.all_to_all(asked, 'node', split_axis=0, concat_axis=0, tiled=True)  4.3 us
    pallas_call x1, Pallas kernels, per_device(): pl.pallas_call(state_kernel, out_shape=pltpu.HBM((4, width, rows), f32),...  3.79 us
  transfers between devices with their start and end apart: 9, of which 4 were waited for; matrix products, arithmetic and copies ran while one was open for 4% of the time, Pallas kernels for 38%

profile of v4, /device:TPU:0, one launch (start us, length us, event | category | flops | bytes accessed | tf_op | source)
XLA Modules:
  0.0 91.2 jit_solution(8356578566946649814)
XLA Ops:
  0.6 0.7 reduce
  1.3 0.7 reshape.44
  2.0 7.3 %all-to-all-start = ((s32[8,1,192]{2,1,0:T(1,128)}), s32[8,1,192]{2,1,0:T(1,128)S(1)}, u32[]{:S(2)}, u32[]{:S(2)}) async-start(s32[8,1,192]{2,1,0:T(1,128)} %reshape.44), calls=%async_computation | async-start | bytes 16384 | tf_op jit(solution)/shard_map/all_to_all | solution.py:423
  9.3 0.7 copy-done.1
  10.0 1.5 %pack.1 = (bf16[176,1024]{1,0:T(8,128)(2,1)S(1)}, bf16[976,128]{1,0:T(8,128)(2,1)S(1)}, bf16[976,128]{1,0:T(8,128)(2,1)S(1)}, bf16[976,128]{1,0:T(8,128)(2,1)S(1)}, bf16[976,128]{1,0:T(8,128)(2,1)S(1)}) custom-call(s32[1]{0:T(128)} %bitcast.feat_ref, bf16[64,2048]{1,0:T(8,128)(2,1)} %bitcast.40, f32[3,43,700]{2,1,0:T(8,128)} %bitcast.38, ...), custom_call_target="tpu_custom_call" | custom-call | flops 100000000 | bytes 1000000 | tf_op jit(solution)/shard_map/pack/pallas_call | solution.py:438
  11.6 4.3 %all-to-all-done = s32[8,1,192]{2,1,0:T(1,128)S(1)} async-done(((s32[8,1,192]{2,1,0:T(1,128)}), s32[8,1,192]{2,1,0:T(1,128)S(1)}, u32[]{:S(2)}, u32[]{:S(2)}) %all-to-all-start) | async-done | bytes 6176 | tf_op jit(solution)/shard_map/all_to_all | solution.py:423
  15.9 1.6 %rows.1 = bf16[8,264,128]{2,1,0:T(8,128)(2,1)} custom-call(s32[8,192]{1,0:T(8,128)S(1)} %bitcast.27, bf16[176,1024]{1,0:T(8,128)(2,1)S(1)} %get-tuple-element.19.table_ref), custom_call_target="tpu_custom_call" | custom-call | flops 1000000000 | bytes 2000000 | tf_op jit(solution)/shard_map/rows/pallas_call | solution.py:455
  17.5 3.5 %all-to-all-start.1 = ((bf16[8,264,128]{2,1,0:T(8,128)(2,1)}), bf16[8,264,128]{2,1,0:T(8,128)(2,1)S(1)}, u32[]{:S(2)}, u32[]{:S(2)}) async-start(bf16[8,264,128]{2,1,0:T(8,128)(2,1)} %rows.1), calls=%async_computation.1 | async-start | bytes 1081344 | tf_op jit(solution)/shard_map/all_to_all | solution.py:464
  21.0 0.1 collective-permute-start.3
  21.1 1.6 %collective-permute-start.4 = (bf16[976,128]{1,0:T(8,128)(2,1)S(1)}, bf16[976,128]{1,0:T(8,128)(2,1)S(1)}, u32[]{:S(2)}, u32[]{:S(2)}) collective-permute-start(bf16[976,128]{1,0:T(8,128)(2,1)S(1)} %get-tuple-element.23), channel_id=1, source_target_pairs={{0,2},{1,3},{2,0},{3,1},{4,6},{5,7},{6,4},{7,5},{8,10},{9,11},{10,... | collective-permute-start | bytes 749576 | tf_op jit(solution)/shard_map/ppermute | solution.py:449
  22.7 1.4 %collective-permute-start.5 = (bf16[976,128]{1,0:T(8,128)(2,1)S(1)}, bf16[976,128]{1,0:T(8,128)(2,1)S(1)}, u32[]{:S(2)}, u32[]{:S(2)}) collective-permute-start(bf16[976,128]{1,0:T(8,128)(2,1)S(1)} %get-tuple-element.24), channel_id=1, source_target_pairs={{0,3},{1,0},{2,1},{3,2},{4,7},{5,4},{6,5},{7,6},{8,11},{9,8},{10,9... | collective-permute-start | bytes 749576 | tf_op jit(solution)/shard_map/ppermute | solution.py:449
  24.1 0.0 copy-done.9
  24.1 0.1 copy.30
  24.2 0.0 collective-permute-start.2
  24.2 0.0 copy-start.7
  24.2 0.0 copy-start.8
  24.2 0.0 copy-start
  24.2 0.0 copy-start.2
  24.2 3.8 %state.1.state_hbm = f32[4,43,1024]{2,1,0:T(8,128)} custom-call(f32[172,1024]{1,0:T(8,128)} %bitcast.37, f32[3,43,700]{2,1,0:T(8,128)} %bitcast.39, f32[3,43,172]{2,1,0:T(8,128)} %bitcast.49, f32[43,4]{1,0:T(8,128)S(1)} %bitcast.31), custom_call_target="tpu_custom_call" | custom-call | flops 3000000000 | bytes 3000000 | tf_op jit(solution)/shard_map/state/pallas_call | solution.py:466
  28.0 0.7 collective-permute-start.1
  28.8 5.2 %collective-permute-done.2 = s32[8,192]{1,0:T(8,128)S(1)} collective-permute-done((s32[8,192]{1,0:T(8,128)S(1)}, s32[8,192]{1,0:T(8,128)S(1)}, u32[]{:S(2)}, u32[]{:S(2)}) %collective-permute-start.2) | collective-permute-done | bytes 6176 | tf_op jit(solution)/shard_map/ppermute | solution.py:482
  34.0 0.8 collective-permute-start
  34.8 1.6 %dynamic-slice_bitcast_fusion.own_hbm = f32[43,1024]{1,0:T(8,128)} fusion(f32[1024,172]{0,1:T(8,128)} %param.19, s32[]{:T(128)S(6)} %select_n.3), kind=kLoop, calls=%fused_computation | loop fusion | bytes 352260 | tf_op jit(solution)/shard_map/dynamic_slice | solution.py:481
  36.4 0.0 copy-done.7
  36.4 0.1 pad.7.freq_ref
  36.5 0.1 pad.8.phase_ref
  36.6 0.1 copy.33.freq_ref
  36.7 0.1 copy.34.phase_ref
  36.8 0.0 collective-permute-done.1
  36.8 0.4 collective-permute-done
  37.3 0.1 reshape.50
  37.4 0.0 all-to-all-done.1.rows_ref
  37.4 0.0 collective-permute-done.3.rest_refs_1_
  37.4 0.0 collective-permute-done.4.rest_refs_2_
  37.4 0.0 collective-permute-done.5.rest_refs_3_
  37.4 5.2 %messages.1 = (bf16[256,1536]{1,0:T(8,128)(2,1)}, bf16[32,200,128]{2,1,0:T(8,128)(2,1)}) custom-call(s32[1]{0:T(128)} %bitcast.feat_ref, bf16[8,264,128]{2,1,0:T(8,128)(2,1)S(1)} %all-to-all-done.1.rows_ref, s32[12,512]{1,0:T(8,128)S(1)} %bitcast.26, s32[1,512]{1,0:T(1,128)S(1)} %bitcast.33, f32[100,1]{1,0:T(8,128)S(1)} %copy.33.freq_ref, ...), custom_call_target="tpu_custom_call" | custom-call | flops 4000000000 | bytes 4000000 | tf_op jit(solution)/shard_map/messages/pallas_call | solution.py:493
  42.7 0.0 copy-start.6
  42.7 0.0 copy-start.5
  42.7 0.0 copy-start.3
  42.7 0.0 copy-start.4
  42.7 5.7 %all-to-all-start.2 = ((bf16[32,200,128]{2,1,0:T(8,128)(2,1)}), bf16[32,200,128]{2,1,0:T(8,128)(2,1)S(1)}, u32[]{:S(2)}, u32[]{:S(2)}) async-start(bf16[32,200,128]{2,1,0:T(8,128)(2,1)} %get-tuple-element.28), calls=%async_computation.2 | async-start | bytes 3276800 | tf_op jit(solution)/shard_map/all_to_all | solution.py:519
  48.4 0.1 copy.35.ref_ref
  48.6 0.1 copy.36.gap_ref
  48.7 0.1 copy.37.wm_ref
  48.9 29.7 %embed.1 = bf16[512,172]{1,0:T(8,128)(2,1)S(1)} custom-call(bf16[256,1536]{1,0:T(8,128)(2,1)} %get-tuple-element.25.table_ref, s32[512,12]{1,0:T(8,128)S(1)} %copy.35.ref_ref, s32[512,10]{1,0:T(8,128)S(1)} %copy.36.gap_ref, f32[1,256]{1,0:T(1,128)S(1)} %pad.7.freq_ref, f32[1,256]{1,0:T(1,128)S(1)} %pad.8.phase_ref, bf16[272,272]{1,0:T(8,128)(2,1)} %wq_ref.1, ...), custom_call_target="tpu_custom_call" | custom-call | flops 20000000000 | bytes 4000000 | tf_op jit(solution)/shard_map/embed/pallas_call | solution.py:523
  78.6 0.8 copy.38
  79.4 7.9 %all-to-all-done.2.recv_ref = bf16[32,200,128]{2,1,0:T(8,128)(2,1)S(1)} async-done(((bf16[32,200,128]{2,1,0:T(8,128)(2,1)}), bf16[32,200,128]{2,1,0:T(8,128)(2,1)S(1)}, u32[]{:S(2)}, u32[]{:S(2)}) %all-to-all-start.2) | async-done | bytes 1638432 | tf_op jit(solution)/shard_map/all_to_all | solution.py:519
  87.3 3.7 %update.1 = f32[43,1024]{1,0:T(8,128)} custom-call(s32[1]{0:T(128)} %bitcast.feat_ref, bf16[32,200,128]{2,1,0:T(8,128)(2,1)S(1)} %all-to-all-done.2.recv_ref, s32[8,1,768]{2,1,0:T(1,128)S(1)} %pad_add_fusion.1.ids_ref, f32[4,43,1024]{2,1,0:T(8,128)} %state.1.state_hbm, f32[43,1024]{1,0:T(8,128)} %dynamic-slice_bitcast_fusion.own_hbm), custom_call_target="tpu_custom_call" | custom-call | flops 4000000000 | bytes 4000000 | tf_op jit(solution)/shard_map/update/pallas_call | solution.py:565
  (16 shorter events, 0.1 us)
Async XLA Ops:
  2.0 13.8 %all-to-all-start = ((s32[8,1,192]{2,1,0:T(1,128)}), s32[8,1,192]{2,1,0:T(1,128)S(1)}, u32[]{:S(2)}, u32[]{:S(2)}) async-start(s32[8,1,192]{2,1,0:T(1,128)} %reshape.44), calls=%async_computation | async-start | bytes 16384 | tf_op jit(solution)/shard_map/all_to_all | solution.py:423
  9.3 0.7 copy-start.1
  15.9 8.2 %copy-start.9 = (f32[4,43]{1,0:T(4,128)S(1)}, f32[4,43]{1,0:T(4,128)}, u32[]{:S(2)}) copy-start(f32[4,43]{1,0:T(4,128)} %param.37) | copy-start | bytes 2068
  17.5 19.9 %all-to-all-start.1 = ((bf16[8,264,128]{2,1,0:T(8,128)(2,1)}), bf16[8,264,128]{2,1,0:T(8,128)(2,1)S(1)}, u32[]{:S(2)}, u32[]{:S(2)}) async-start(bf16[8,264,128]{2,1,0:T(8,128)(2,1)} %rows.1), calls=%async_computation.1 | async-start | bytes 1081344 | tf_op jit(solution)/shard_map/all_to_all | solution.py:464
  21.0 16.3 %collective-permute-start.3 = (bf16[976,128]{1,0:T(8,128)(2,1)S(1)}, bf16[976,128]{1,0:T(8,128)(2,1)S(1)}, u32[]{:S(2)}, u32[]{:S(2)}) collective-permute-start(bf16[976,128]{1,0:T(8,128)(2,1)S(1)} %get-tuple-element.22), channel_id=1, source_target_pairs={{0,1},{1,2},{2,3},{3,0},{4,5},{5,6},{6,7},{7,4},{8,9},{9,10},{10,1... | collective-permute-start | bytes 749576 | tf_op jit(solution)/shard_map/ppermute | solution.py:449
  21.1 16.3 %collective-permute-start.4 = (bf16[976,128]{1,0:T(8,128)(2,1)S(1)}, bf16[976,128]{1,0:T(8,128)(2,1)S(1)}, u32[]{:S(2)}, u32[]{:S(2)}) collective-permute-start(bf16[976,128]{1,0:T(8,128)(2,1)S(1)} %get-tuple-element.23), channel_id=1, source_target_pairs={{0,2},{1,3},{2,0},{3,1},{4,6},{5,7},{6,4},{7,5},{8,10},{9,11},{10,... | collective-permute-start | bytes 749576 | tf_op jit(solution)/shard_map/ppermute | solution.py:449
  22.7 14.7 %collective-permute-start.5 = (bf16[976,128]{1,0:T(8,128)(2,1)S(1)}, bf16[976,128]{1,0:T(8,128)(2,1)S(1)}, u32[]{:S(2)}, u32[]{:S(2)}) collective-permute-start(bf16[976,128]{1,0:T(8,128)(2,1)S(1)} %get-tuple-element.24), channel_id=1, source_target_pairs={{0,3},{1,0},{2,1},{3,2},{4,7},{5,4},{6,5},{7,6},{8,11},{9,8},{10,9... | collective-permute-start | bytes 749576 | tf_op jit(solution)/shard_map/ppermute | solution.py:449
  24.2 9.8 %collective-permute-start.2 = (s32[8,192]{1,0:T(8,128)S(1)}, s32[8,192]{1,0:T(8,128)S(1)}, u32[]{:S(2)}, u32[]{:S(2)}) collective-permute-start(s32[8,192]{1,0:T(8,128)S(1)} %bitcast.28), channel_id=1, source_target_pairs={{0,3},{1,0},{2,1},{3,2},{4,7},{5,4},{6,5},{7,6},{8,11},{9,8},{10,9... | collective-permute-start | bytes 18440 | tf_op jit(solution)/shard_map/ppermute | solution.py:482
  24.2 12.2 %copy-start.7 = (f32[100]{0:T(128)S(1)}, f32[100]{0:T(128)}, u32[]{:S(2)}) copy-start(f32[100]{0:T(128)} %param.26) | copy-start | bytes 1204
  24.2 12.3 %copy-start.8 = (f32[100]{0:T(128)S(1)}, f32[100]{0:T(128)}, u32[]{:S(2)}) copy-start(f32[100]{0:T(128)} %param.27) | copy-start | bytes 1204
  24.2 13.2 %copy-start = (s32[512,12]{0,1:T(8,128)S(1)}, s32[512,12]{0,1:T(8,128)}, u32[]{:S(2)}) copy-start(s32[512,12]{0,1:T(8,128)} %param.24) | copy-start | bytes 73732
  24.2 13.2 %copy-start.2 = (s32[512]{0:T(512)S(1)}, s32[512]{0:T(512)}, u32[]{:S(2)}) copy-start(s32[512]{0:T(512)} %param.21) | copy-start | bytes 6148
  28.0 8.8 %collective-permute-start.1 = (s32[8,192]{1,0:T(8,128)S(1)}, s32[8,192]{1,0:T(8,128)S(1)}, u32[]{:S(2)}, u32[]{:S(2)}) collective-permute-start(s32[8,192]{1,0:T(8,128)S(1)} %bitcast.29), channel_id=1, source_target_pairs={{0,2},{1,3},{2,0},{3,1},{4,6},{5,7},{6,4},{7,5},{8,10},{9,11},{10,... | collective-permute-start | bytes 18440 | tf_op jit(solution)/shard_map/ppermute | solution.py:482
  34.0 3.2 %collective-permute-start = (s32[8,192]{1,0:T(8,128)S(1)}, s32[8,192]{1,0:T(8,128)S(1)}, u32[]{:S(2)}, u32[]{:S(2)}) collective-permute-start(s32[8,192]{1,0:T(8,128)S(1)} %bitcast.30), channel_id=1, source_target_pairs={{0,1},{1,2},{2,3},{3,0},{4,5},{5,6},{6,7},{7,4},{8,9},{9,10},{10,1... | collective-permute-start | bytes 18440 | tf_op jit(solution)/shard_map/ppermute | solution.py:482
  42.7 5.9 %copy-start.6 = (s32[512,10]{0,1:T(8,128)S(1)}, s32[512,10]{0,1:T(8,128)}, u32[]{:S(2)}) copy-start(s32[512,10]{0,1:T(8,128)} %param.22) | copy-start | bytes 61444
  42.7 6.0 %copy-start.5 = (bf16[444,172]{0,1:T(8,128)(2,1)S(1)}, bf16[444,172]{0,1:T(8,128)(2,1)}, u32[]{:S(2)}) copy-start(bf16[444,172]{0,1:T(8,128)(2,1)} %param.31) | copy-start | bytes 458212
  42.7 6.2 %copy-start.3 = (f32[172]{0:T(256)S(1)}, f32[172]{0:T(256)}, u32[]{:S(2)}) copy-start(f32[172]{0:T(256)} %param.32) | copy-start | bytes 2068
  42.7 6.2 %copy-start.4 = (f32[172]{0:T(256)S(1)}, f32[172]{0:T(256)}, u32[]{:S(2)}) copy-start(f32[172]{0:T(256)} %param.34) | copy-start | bytes 2068
  42.7 44.6 %all-to-all-start.2 = ((bf16[32,200,128]{2,1,0:T(8,128)(2,1)}), bf16[32,200,128]{2,1,0:T(8,128)(2,1)S(1)}, u32[]{:S(2)}, u32[]{:S(2)}) async-start(bf16[32,200,128]{2,1,0:T(8,128)(2,1)} %get-tuple-element.28), calls=%async_computation.2 | async-start | bytes 3276800 | tf_op jit(solution)/shard_map/all_to_all | solution.py:519
